TPU v7x, 32 devices: a whole 2x2x4 slice. The times are simulated.
32 devices in a mesh: row: 4 (over x, core), col: 8 (over z, y).
Axes of the slice: x: 2, y: 2, z: 4, core: 2. Of those that a mesh axis runs over, the one named last changes fastest.
Arguments:
- panel_rows: float32 [4096, 4096], P('row', 'col'), may hold values from -0.75 to 0.75
- owner_slot: int32 [8, 8], replicated, may hold values from -1 to 15, as said below
Outputs:
- packed: float32 [4, 16, 512, 512], P('row', 'col')
Inputs may be any that keep to these rules, and one draw needn't show every extreme that they name: For j <= i, owner_slot[i, j] is the position of tile (i, j) among the 16 positions of group i // 2; tiles of one group have distinct positions; entries above the diagonal are -1. Position p lies on the device of col index p // 2.
All inputs are finite; a program needn't handle non-finite values.
Results may differ from a plain program's by a relative error of at most 0.0003.
Values sent between devices are 32-bit elements; how exact they have to be, the bound alone decides.
No kernel may reach another device: no remote copies, remote signals or barrier semaphores. Data moves between devices by JAX's collectives and lax.ppermute only.
A program may use at most 128 MiB of HBM per device.

v0:
```python
import jax
import jax.numpy as jnp
from jax import lax
from jax.sharding import PartitionSpec as P

BLOCK = 512


def slot_table(owner_slot, group_id, positions, per_group):
    blocks = owner_slot.shape[0]
    block_row = jnp.arange(blocks, dtype=jnp.int32)[:, None]
    block_col = jnp.arange(blocks, dtype=jnp.int32)[None, :]
    inside = (block_row // per_group == group_id) & (block_col <= block_row)
    wanted = jnp.arange(positions, dtype=jnp.int32)[:, None, None]
    matched = inside[None] & (owner_slot[None] == wanted)
    is_live = jnp.any(matched, axis=(1, 2))
    left_block = jnp.sum(jnp.where(matched, block_row[None], 0), axis=(1, 2))
    right_block = jnp.sum(jnp.where(matched, block_col[None], 0), axis=(1, 2))
    return (left_block, right_block, is_live)


def tile_products(tiles_all, lefts, rights, flags):

    def single(packed_item):
        left_one, right_one, flag = packed_item

        def compute():
            return lax.dot_general(
                tiles_all[left_one],
                tiles_all[right_one],
                (((1,), (1,)), ((), ())),
                precision=lax.Precision.HIGHEST,
                preferred_element_type=jnp.float32,
            )

        def blank():
            return jnp.zeros((BLOCK, BLOCK), jnp.float32)

        return lax.cond(flag, compute, blank)

    return lax.map(single, (lefts, rights, flags))


def body(panel_rows, owner_slot):
    rows_n = lax.axis_size("row")
    cols_n = lax.axis_size("col")
    slab_rows, inner_cols = panel_rows.shape
    per_group = slab_rows // BLOCK
    blocks = per_group * rows_n
    row_tiles = per_group * (blocks - per_group) + per_group * (per_group + 1) // 2
    slot_count = (row_tiles + cols_n - 1) // cols_n
    positions = cols_n * slot_count
    gathered = lax.all_gather(panel_rows, "row", axis=0, tiled=True)
    my_group = lax.axis_index("row")
    left_block, right_block, is_live = slot_table(owner_slot, my_group, positions, per_group)
    tiles_all = gathered.reshape(blocks, BLOCK, inner_cols)
    summed = lax.psum_scatter(
        tile_products(tiles_all, left_block, right_block, is_live),
        "col",
        scatter_dimension=0,
        tiled=True,
    )
    return summed[None]


def solution(mesh):
    placed = (P("row", "col"), P())
    return jax.shard_map(
        body, mesh=mesh, in_specs=placed, out_specs=P("row", "col", None, None), check_vma=False
    )
```

profile of v0, /device:TPU:0, one launch (start us, length us, event | category | flops | bytes accessed | tf_op | source)
XLA Modules:
  0.0 511.2 jit_solution(8440207610990684150)
XLA Ops:
  6.5 0.7 all-gather.2.cloned.1.call-update
  7.4 0.8 select_reduce_fusion
  8.2 0.8 fusion.6
  9.0 60.9 %all-gather.2.cloned.1.call-done = f32[4096,512]{1,0:T(8,128)} async-done(((f32[1024,512]{1,0:T(8,128)}), f32[4096,512]{1,0:T(8,128)}) %all-gather.2.cloned.1.call-update) | async-done | bytes 8388624 | tf_op jit(solution)/shard_map/all_gather | solution.py:53
  69.9 61.2 %while.10 = (s32[]{:T(128)}, f32[16,512,512]{2,1,0:T(8,128)}, pred[16]{0:T(512)(128)(4,1)S(1)}, s32[16]{0:T(128)S(1)}, f32[8,512,512]{2,1,0:T(8,128)}, /*index=5*/s32[16]{0:T(128)S(1)}, s32[]{:T(128)}) while((s32[]{:T(128)}, f32[16,512,512]{2,1,0:T(8,128)}, pred[16]{0:T(512)(128)(4,1)S(1)}, s32[16]{0:T(128)S(1)}, f32[8,512,512]{2,1,0:T(8,128)}, ...), condition=%wide.region_6.7_spmd, body=%wide.region_3.6_spmd.sunk | while | flops 1610612736 | bytes 5243620 | solution.py:41
  69.9 0.6 dynamic_slice.32
  71.0 0.1 conditional.2
  71.2 1.1 constant_dynamic-update-slice_fusion.2
  72.3 0.6 dynamic_slice.32
  73.4 0.1 conditional.2
  73.5 1.1 constant_dynamic-update-slice_fusion.2
  74.7 0.6 dynamic_slice.32
  75.8 7.9 %conditional.2 = (f32[1,512,512]{2,1,0:T(8,128)S(1)}) conditional(s32[]{:T(128)} %bitcast.14, () %tuple.31, (s32[16]{0:T(128)S(1)}, s32[]{:T(128)}, f32[8,512,512]{2,1,0:T(8,128)}, s32[16]{0:T(128)S(1)}) %tuple.32), branch_computations={%region_4.4_spmd, %region_5.5_spmd} | conditional | flops 1610612736 | bytes 3145836 | solution.py:39
  75.8 0.6 dynamic_slice.18
  78.1 0.6 dynamic_slice.20
  80.3 3.4 convolution_bitcast_fusion
  83.7 1.1 constant_dynamic-update-slice_fusion.2
  84.8 0.6 dynamic_slice.32
  85.9 0.1 conditional.2
  86.1 1.1 constant_dynamic-update-slice_fusion.2
  87.1 0.6 dynamic_slice.32
  88.3 0.1 conditional.2
  88.4 1.0 constant_dynamic-update-slice_fusion.2
  89.5 0.6 dynamic_slice.32
  90.6 0.1 conditional.2
  90.6 0.1 broadcast_in_dim.35
  90.8 1.1 constant_dynamic-update-slice_fusion.2
  91.9 0.6 dynamic_slice.32
  93.0 0.1 conditional.2
  93.1 1.1 constant_dynamic-update-slice_fusion.2
  94.2 0.6 dynamic_slice.32
  95.4 0.1 conditional.2
  95.5 1.0 constant_dynamic-update-slice_fusion.2
  96.6 0.6 dynamic_slice.32
  97.7 0.1 conditional.2
  97.8 1.1 constant_dynamic-update-slice_fusion.2
  99.0 0.6 dynamic_slice.32
  100.1 0.1 conditional.2
  100.3 1.0 constant_dynamic-update-slice_fusion.2
  101.3 0.6 dynamic_slice.32
  102.5 0.1 conditional.2
  102.6 1.1 constant_dynamic-update-slice_fusion.2
  103.7 0.6 dynamic_slice.32
  104.8 0.1 conditional.2
  104.9 1.0 constant_dynamic-update-slice_fusion.2
  106.0 0.6 dynamic_slice.32
  107.1 0.1 conditional.2
  107.3 1.1 constant_dynamic-update-slice_fusion.2
  108.4 0.6 dynamic_slice.32
  109.5 0.1 conditional.2
  109.7 1.0 constant_dynamic-update-slice_fusion.2
  110.7 0.6 dynamic_slice.32
  111.9 8.0 %conditional.2 = (f32[1,512,512]{2,1,0:T(8,128)S(1)}) conditional(s32[]{:T(128)} %bitcast.14, () %tuple.31, (s32[16]{0:T(128)S(1)}, s32[]{:T(128)}, f32[8,512,512]{2,1,0:T(8,128)}, s32[16]{0:T(128)S(1)}) %tuple.32), branch_computations={%region_4.4_spmd, %region_5.5_spmd} | conditional | flops 1610612736 | bytes 3145836 | solution.py:39
  111.9 0.6 dynamic_slice.18
  114.2 0.6 dynamic_slice.20
  116.4 3.5 convolution_bitcast_fusion
  119.9 1.1 constant_dynamic-update-slice_fusion.2
  121.0 0.6 dynamic_slice.32
  122.1 8.0 %conditional.2 = (f32[1,512,512]{2,1,0:T(8,128)S(1)}) conditional(s32[]{:T(128)} %bitcast.14, () %tuple.31, (s32[16]{0:T(128)S(1)}, s32[]{:T(128)}, f32[8,512,512]{2,1,0:T(8,128)}, s32[16]{0:T(128)S(1)}) %tuple.32), branch_computations={%region_4.4_spmd, %region_5.5_spmd} | conditional | flops 1610612736 | bytes 3145836 | solution.py:39
  122.1 0.6 dynamic_slice.18
  124.4 0.6 dynamic_slice.20
  126.6 3.4 convolution_bitcast_fusion
  130.1 1.1 constant_dynamic-update-slice_fusion.2
  131.2 373.2 %reduce-scatter.2.cloned.1.call-done = f32[2,512,512]{2,1,0:T(8,128)} async-done(((f32[16,512,512]{2,1,0:T(8,128)}), f32[2,512,512]{2,1,0:T(8,128)}) %reduce-scatter.2.cloned.1.call-update) | async-done | bytes 2097168 | tf_op jit(solution)/shard_map/reduce_scatter | solution.py:57
  (18 shorter events, 1.5 us)
Async XLA Ops:
  6.5 63.4 %all-gather.2.cloned.1.call-start = ((), (), s32[]{:S(2)}) async-start(), calls=%async_computation.1 | async-start | bytes 10485760 | tf_op jit(solution)/shard_map/all_gather | solution.py:53
  7.3 497.1 %reduce-scatter.2.cloned.1.call-start = ((), (), s32[]{:S(2)}) async-start(), calls=%async_computation.2 | async-start | bytes 18874368 | tf_op jit(solution)/shard_map/reduce_scatter | solution.py:57
Sparse Core Ops, SparseCore 0:
  8.9 60.9 all-gather.1
  131.3 373.0 reduce-scatter.1
where the time goes:
time: 513 us; the launch traced here: 511 us
  waiting for transfers between devices  435 us (85%)
  local copies, waits for them, and re-layouts  31.4 us (6%)
  loops' own time  19.6 us (4%)
  between operations  13.4 us (3%)
  matrix products  10.3 us (2%)
    reduce_scatter x1, waiting for transfers between devices, body(): lax.psum_scatter(tile_products(tiles_all, left_block, right_block, is_liv...  373 us
    all_gather x1, waiting for transfers between devices, body(): gathered = lax.all_gather(panel_rows, 'row', axis=0, tiled=True)  60.9 us
    dynamic_update_slice x16, local copies, waits for them, and re-layouts, tile_products(): return lax.map(single, (lefts, rights, flags))  17.1 us
    dynamic_slice x22, local copies, waits for them, and re-layouts, tile_products(): return lax.map(single, (lefts, rights, flags))  12.7 us
    another operation x16, loops' own time, single(): return lax.cond(flag, compute, blank)  10.4 us
    dot_general x3, matrix products, compute(): lax.dot_general(tiles_all[left_one], tiles_all[right_one], (((1,), (1,)),...  10.3 us
  transfers between devices with their start and end apart: 2, of which 2 were waited for; matrix products, arithmetic and copies ran while one was open for 0% of the time, Pallas kernels for 0%

commit v1 on v0

v1 whole, which is shorter than its diff:
```python
import functools

import jax
import jax.numpy as jnp
from jax import lax
from jax.experimental import pallas as pl
from jax.experimental.pallas import tpu as pltpu
from jax.sharding import Mesh, PartitionSpec as P

BLOCK = 512
WIDE = 256


def split_hi_lo(x):
    hi = x.astype(jnp.bfloat16)
    lo = (x - hi.astype(jnp.float32)).astype(jnp.bfloat16)
    return hi, lo


def product_kernel(dims, outs, meta_ref, pairs_ref, index_ref, s_ref, *refs):
    blocks, h, kc, ys, rb, cb, n_pairs = dims
    pieces, lists, (s_cat, j_cat, part) = refs[:4], refs[4 : 4 + outs], refs[4 + outs :]
    core = meta_ref[0]
    q = h // 2

    def put(target, row, y, x, right):
        hi, lo = split_hi_lo(x)
        base = 3 * kc * y
        rows = pl.ds(pl.multiple_of(row, q), x.shape[0])
        target[rows, base : base + kc] = hi
        target[rows, base + kc : base + 2 * kc] = lo if right else hi
        target[rows, base + 2 * kc : base + 3 * kc] = hi if right else lo

    @pl.loop(0, blocks)
    def _(j):
        for y in range(ys):
            put(s_cat, j * h, y, s_ref[y, j], False)
            for at, piece in enumerate(pieces):
                side = core if at % 2 == 0 else 1 - core
                put(j_cat, j * 2 * h + (at // 2 * 2 + side) * q, y, piece[y, j], True)

    @pl.loop(0, n_pairs)
    def _(t):
        ib, jb = pairs_ref[2 * t], pairs_ref[2 * t + 1]
        left = s_cat[pl.ds(pl.multiple_of(ib * rb, rb), rb), :]
        right = j_cat[pl.ds(pl.multiple_of(jb * cb, cb), cb), :]
        out = lax.dot_general(left, right, (((1,), (1,)), ((), ())), preferred_element_type=jnp.float32)
        for a in range(rb // h):
            for b in range(cb // (2 * h)):
                where = (ib * (rb // h) + a) * blocks + jb * (cb // (2 * h)) + b
                part[where] = out[a * h : (a + 1) * h, b * 2 * h : (b + 1) * 2 * h]

    @pl.loop(0, lists[0].shape[0])
    def _(k):
        for at, one in enumerate(lists):
            one[k] = part[index_ref[at * one.shape[0] + k]]


def products(dims, outs, n, meta, pairs, index, s, pieces):
    blocks, h, kc, ys, rb, cb, n_pairs = dims
    k3 = 3 * kc * ys
    smem, vmem = pl.BlockSpec(memory_space=pltpu.SMEM), pl.BlockSpec(memory_space=pltpu.VMEM)
    flops = 2 * n_pairs * rb * cb * k3
    return pl.pallas_call(
        functools.partial(product_kernel, dims, outs),
        out_shape=[jax.ShapeDtypeStruct((n, h, 2 * h), jnp.float32)] * outs,
        in_specs=[smem] * 3 + [vmem] * 5,
        out_specs=[vmem] * outs,
        scratch_shapes=[
            pltpu.VMEM((blocks * h, k3), jnp.bfloat16),
            pltpu.VMEM((blocks * 2 * h, k3), jnp.bfloat16),
            pltpu.VMEM((blocks * blocks, h, 2 * h), jnp.float32),
        ],
        cost_estimate=pl.CostEstimate(flops=flops, bytes_accessed=8 * s.size * 4, transcendentals=0),
    )(meta, pairs, index, s, *pieces)


def relay_kernel(up_ref, up_list_ref, down_ref, down_list_ref, up_out, down_out):
    up_out[...] = up_ref[...] + up_list_ref[...]
    down_out[...] = down_ref[...] + down_list_ref[...]


def relay(up, up_list, down, down_list):
    vmem = pl.BlockSpec(memory_space=pltpu.VMEM)
    return pl.pallas_call(
        relay_kernel,
        out_shape=[jax.ShapeDtypeStruct(up.shape, jnp.float32)] * 2,
        in_specs=[vmem] * 4,
        out_specs=[vmem] * 2,
        cost_estimate=pl.CostEstimate(flops=2 * up.size, bytes_accessed=24 * up.size, transcendentals=0),
    )(up, up_list, down, down_list)


def pick_kernel(spread_ref, live_ref, *refs):
    out_ref = refs[-1]
    devices, chunks, slots = out_ref.shape[:3]

    @pl.loop(0, devices)
    def _(d):
        for slot in range(slots):
            k = spread_ref[d * slots + slot]
            used = live_ref[d * slots + slot] > 0
            for c in range(chunks):
                total = refs[3 * c][k] + refs[3 * c + 1][k] + refs[3 * c + 2][k]
                out_ref[d, c, slot] = jnp.where(used, total, jnp.zeros_like(total))


def pick(plane, slots, spread, live, terms):
    smem, vmem = pl.BlockSpec(memory_space=pltpu.SMEM), pl.BlockSpec(memory_space=pltpu.VMEM)
    shape = (plane, len(terms) // 3, slots) + terms[0].shape[1:]
    return pl.pallas_call(
        pick_kernel,
        out_shape=jax.ShapeDtypeStruct(shape, jnp.float32),
        in_specs=[smem] * 2 + [vmem] * len(terms),
        out_specs=vmem,
    )(spread, live, *terms)


def place_kernel(plan, in_ref, out_ref):
    h, w = in_ref.shape[3:]
    q = h // 2
    for source, chip, side, parts in plan:
        for col, (first, second) in parts:
            cols = slice(col * w, (col + 1) * w)
            for half in range(2):
                row = chip * w + half * h + side * q
                rows = slice(half * q, (half + 1) * q)
                if first[0] == second[0]:
                    out_ref[:, row : row + q, cols] = in_ref[source, first[0], :, rows, :]
                else:
                    left = in_ref[source, first[0], :, rows, first[1] * h : (first[1] + 1) * h]
                    right = in_ref[source, second[0], :, rows, second[1] * h : (second[1] + 1) * h]
                    out_ref[:, row : row + q, cols] = jnp.concatenate([left, right], axis=2)


def place(plan, arrived):
    vmem = pl.BlockSpec(memory_space=pltpu.VMEM)
    return pl.pallas_call(
        functools.partial(place_kernel, plan),
        out_shape=jax.ShapeDtypeStruct((arrived.shape[2], BLOCK, BLOCK), jnp.float32),
        in_specs=[vmem],
        out_specs=vmem,
    )(arrived)


def list_tables(owner_slot, rows_n, zs, ys, slots, per_group):
    blocks = owner_slot.shape[0]
    positions = zs * ys * slots
    block_row = jnp.arange(blocks, dtype=jnp.int32)[:, None]
    block_col = jnp.arange(blocks, dtype=jnp.int32)[None, :]
    inside = block_col <= block_row
    wanted = jnp.arange(positions, dtype=jnp.int32)
    matched = (inside[None] & (owner_slot[None] == wanted[:, None, None])).reshape(positions, rows_n, per_group, blocks)
    tile_id = (block_row * blocks + block_col).reshape(1, rows_n, per_group, blocks)
    tile = jnp.sum(jnp.where(matched, tile_id, 0), axis=(2, 3))
    live = jnp.sum(matched.astype(jnp.int32), axis=(2, 3))
    entries = ys * rows_n * slots

    def by_plane(x):
        return x.reshape(zs, ys, slots, rows_n).transpose(0, 1, 3, 2).reshape(zs, entries)

    tile, live = by_plane(tile), by_plane(live)
    order = jnp.arange(entries, dtype=jnp.int32)
    before = order[None, :, None] > order[None, None, :]
    rank = jnp.sum(jnp.where(before, live[:, None, :], 0), axis=2)
    hit = (rank[:, None, :] == order[None, :, None]) & (live[:, None, :] > 0)
    index = jnp.sum(jnp.where(hit, tile[:, None, :], 0), axis=2)
    longest = jnp.max(jnp.sum(live, axis=1))
    return index, rank, live, longest


def make_plan(chips, zs):
    singles = [u for u in range(1, chips) if u & (u - 1) == 0]
    chunks = [((0, 0), (0, 1))]
    if len(singles) > 1:
        chunks += [((singles[-1], half), (singles[0], half)) for half in range(2)]
    used = {u for chunk in chunks for u, _ in chunk}
    chunks += [((u, 0), (u, 1)) for u in range(1, chips) if u not in used]
    events = []
    for c in range(len(chunks)):
        events.append((3 * c, "product", c, 0))
        events.extend((3 * c + 2.2 * (step - 1), "step", c, step) for step in range(2, zs))
        if c:
            events.append((3 * c - 1.5, "fetch", c, 0))
    events.sort(key=lambda e: e[0])
    return chunks, events


def link_of(u, half):
    return u & -u if half == 0 else 1 << (u.bit_length() - 1)


def body(panel_rows, owner_slot):
    rows_n, zs, ys = (lax.axis_size(name) for name in ("row", "z", "y"))
    slab_rows, kc = panel_rows.shape
    per_group = slab_rows // BLOCK
    blocks = per_group * rows_n
    cols_n = zs * ys
    row_tiles = per_group * (blocks - per_group) + per_group * (per_group + 1) // 2
    slots = (row_tiles + cols_n - 1) // cols_n
    plane = rows_n * ys
    chips = plane // 2
    h = BLOCK // plane
    rb, cb = min(WIDE, blocks * h), min(WIDE, blocks * 2 * h)
    per_i, per_j = rb // h, cb // (2 * h)
    pair_list = [
        (ib, jb)
        for ib in range(blocks // per_i)
        for jb in range(blocks // per_j)
        if ib * per_i + per_i - 1 >= jb * per_j
    ]
    dims = (blocks, h, kc, ys, rb, cb, len(pair_list))
    pairs = jnp.array([v for pair in pair_list for v in pair], jnp.int32)
    my_z, my_row, my_y = (lax.axis_index(name) for name in ("z", "row", "y"))
    meta = jnp.stack([my_row % 2, (my_row // 2) * ys + my_y]).astype(jnp.int32)
    index, rank, live, longest = list_tables(owner_slot, rows_n, zs, ys, slots, per_group)
    entries = ys * rows_n * slots

    steps = range(1, zs)
    wanted = [my_z + zs - step for step in steps] + [my_z - zs + step for step in steps] + [my_z]
    wanted = jnp.clip(jnp.stack(wanted), 0, zs - 1)
    at_plane = (wanted[:, None] == jnp.arange(zs)[None, :])[:, :, None]
    index = jnp.sum(jnp.where(at_plane, index[None], 0), axis=1)
    own = (jnp.arange(zs) == my_z)[:, None]
    my_rank, my_live = (jnp.sum(jnp.where(own, table, 0), axis=0) for table in (rank, live))

    def chip_swap(x, u):
        ux, uy = u // ys, u % ys
        if uy == 0:
            return lax.ppermute(x, "row", [(r, r ^ (2 * ux)) for r in range(rows_n)])
        if ux == 0:
            return lax.ppermute(x, "y", [(y, y ^ uy) for y in range(ys)])
        perm = [(r * ys + y, (r ^ (2 * ux)) * ys + (y ^ uy)) for r in range(rows_n) for y in range(ys)]
        return lax.ppermute(x, ("row", "y"), perm)

    def core_swap(x):
        return lax.ppermute(x, "row", [(r, r ^ 1) for r in range(rows_n)])

    chunks, events = make_plan(chips, zs)

    def run(n, *args):
        return run_scoped(n, *args)

    def run_scoped(n, panel, index, my_rank, my_live):
        sliced = panel.reshape(per_group, rows_n // 2, ys, 2, 2, h // 2, kc).transpose(2, 1, 4, 0, 3, 5, 6)
        sliced = sliced.reshape(plane, per_group, h, kc)
        s = lax.all_to_all(sliced, ("y", "row"), 0, 0, tiled=True).reshape(ys, blocks, h, kc)
        same, peer = {(0, 0): s[:, :, : h // 2], (0, 1): s[:, :, h // 2 :]}, {}

        def cores(u, half):
            peer[u, half] = core_swap(same[u, half])

        def reach(u, half):
            if (u, half) not in same:
                low = link_of(u, half)
                reach(u ^ low, half)
                same[u, half] = chip_swap(same[u ^ low, half], low)

        for half in range(2):
            cores(0, half)
            for u in range(1, chips):
                reach(u, half)
        flat_index = index[:, :n].reshape(-1)
        lists, flows = {}, {}

        def forward(c, step, up, down):
            up = lax.ppermute(up, "z", [(z, z + 1) for z in range(step)])
            down = lax.ppermute(down, "z", [(zs - 1 - z, zs - 2 - z) for z in range(step)])
            flows[c] = (up, down)

        for _, kind, c, step in events:
            if kind == "fetch":
                for u, half in chunks[c]:
                    cores(u, half)
            elif kind == "product":
                pieces = [side[key] for key in chunks[c] for side in (same, peer)]
                lists[c] = products(dims, 2 * zs - 1, n, meta, pairs, flat_index, s, pieces)
                forward(c, 1, lists[c][0], lists[c][zs - 1])
            else:
                up, down = relay(flows[c][0], lists[c][step - 1], flows[c][1], lists[c][zs + step - 2])
                forward(c, step, up, down)

        terms = [x for c in range(len(chunks)) for x in (lists[c][-1], *flows[c])]
        ready = pick(plane, slots, jnp.minimum(my_rank, n - 1), my_live, terms)
        arrived = lax.all_to_all(ready, ("y", "row"), 0, 0, tiled=True)
        plan = []
        for d in range(plane):
            chip = (d % rows_n) // 2 * ys + d // rows_n
            parts = []
            for u in range(chips):
                spots = []
                for half in range(2):
                    c = next(i for i, chunk in enumerate(chunks) if (u, half) in chunk)
                    spots.append((c, chunks[c].index((u, half))))
                parts.append((chip ^ u, tuple(spots)))
            plan.append((d, chip, d % 2, tuple(parts)))
        return place(tuple(plan), arrived)[None]

    mean = (blocks * (blocks + 1) // 2 + zs - 1) // zs
    sizes = sorted({min(entries, mean + extra) for extra in (3,)} | {entries})
    which = sum((longest > size).astype(jnp.int32) for size in sizes[:-1])
    branches = [functools.partial(run, size) for size in sizes]
    return lax.switch(which, branches, panel_rows, index, my_rank, my_live)


def solution(mesh):
    rows_n, cols_n = mesh.shape["row"], mesh.shape["col"]
    ys = 2 if cols_n % 2 == 0 else 1
    fine = Mesh(mesh.devices.reshape(rows_n, cols_n // ys, ys), ("row", "z", "y"))
    return jax.shard_map(
        body,
        mesh=fine,
        in_specs=(P("row", ("z", "y")), P()),
        out_specs=P("row", ("z", "y"), None, None),
        check_vma=False,
    )
```

time: 513 us -> 264 us (0.51)
  waiting for transfers between devices: 435 us -> 61.2 us
  blocking collectives: 0 us -> 62.4 us
  starting transfers between devices: 0.04 us -> 62.2 us
  Pallas kernels: 0 us -> 60.6 us
  local copies, waits for them, and re-layouts: 31.4 us -> 8.03 us
  loops' own time: 19.6 us -> 0.82 us
  between operations: 13.4 us -> 0.69 us
  matrix products: 10.3 us -> 0 us
    reduce_scatter x1 -> x0, waiting for transfers between devices: 373 us -> none  [body(): lax.psum_scatter(tile_products(tiles_all, left_block, right_block, is_liv...]
    all_to_all x0 -> x2, blocking collectives: none -> 62.4 us  [the longest x1 31.6 us: run_scoped(): lax.all_to_all(sliced, ('y', 'row'), 0, 0, tiled=True)]
    ppermute x0 -> x38, starting transfers between devices: none -> 62.2 us  [the longest x12 43.9 us: forward(): up = lax.ppermute(up, 'z', [(z, z + 1) for z in range(step)])]
    ppermute x0 -> x38, waiting for transfers between devices: none -> 61.2 us  [the longest x3 22.2 us: chip_swap(): return lax.ppermute(x, 'y', [(y, y ^ uy) for y in range(ys)])]
    all_gather x1 -> x0, waiting for transfers between devices: 60.9 us -> none  [body(): gathered = lax.all_gather(panel_rows, 'row', axis=0, tiled=True)]
    pallas_call x0 -> x14, Pallas kernels: none -> 60.6 us  [the longest x4 36.2 us: products(): pl.pallas_call(functools.partial(product_kernel, dims, outs), out_shape=[...]
    another operation x17 -> x1, loops' own time: 19.6 us -> 0.82 us  [body(): return lax.switch(which, branches, panel_rows, index, my_rank, my_live)]
    dynamic_update_slice x16 -> x0, local copies, waits for them, and re-layouts: 17.1 us -> none  [tile_products(): return lax.map(single, (lefts, rights, flags))]
  transfers between devices with their start and end apart: 2 -> 38, of which waited for: 2 -> 8; matrix products, arithmetic and copies ran while one was open for 0% -> 1% of each run, Pallas kernels for 0% -> 21%
where the time goes in v1:
time: 264 us; the launch traced here: 259 us
  blocking collectives  62.4 us (24%)
  starting transfers between devices  62.2 us (24%)
  waiting for transfers between devices  61.2 us (23%)
  Pallas kernels  60.6 us (23%)
  local copies, waits for them, and re-layouts  8.03 us (3%)
  other arithmetic  3.07 us (1%)
    ppermute x12, starting transfers between devices, forward(): up = lax.ppermute(up, 'z', [(z, z + 1) for z in range(step)])  43.9 us
    pallas_call x4, Pallas kernels, products(): pl.pallas_call(functools.partial(product_kernel, dims, outs), out_shape=[...  36.2 us
    all_to_all x1, blocking collectives, run_scoped(): lax.all_to_all(sliced, ('y', 'row'), 0, 0, tiled=True)  31.6 us
    all_to_all x1, blocking collectives, run_scoped(): arrived = lax.all_to_all(ready, ('y', 'row'), 0, 0, tiled=True)  30.9 us
    ppermute x3, waiting for transfers between devices, chip_swap(): return lax.ppermute(x, 'y', [(y, y ^ uy) for y in range(ys)])  22.2 us
    ppermute x3, waiting for transfers between devices, chip_swap(): return lax.ppermute(x, 'row', [(r, r ^ 2 * ux) for r in range(rows_n)])  21.2 us
    pallas_call x8, Pallas kernels, relay(): pl.pallas_call(relay_kernel, out_shape=[jax.ShapeDtypeStruct(up.shape, jn...  18.4 us
    ppermute x12, waiting for transfers between devices, forward(): up = lax.ppermute(up, 'z', [(z, z + 1) for z in range(step)])  15.2 us
  transfers between devices with their start and end apart: 38, of which 8 were waited for; matrix products, arithmetic and copies ran while one was open for 1% of the time, Pallas kernels for 21%

profile of v1, /device:TPU:0, one launch (start us, length us, event | category | flops | bytes accessed | tf_op | source)
XLA Modules:
  0.0 259.1 jit_solution(16269067075304180966)
XLA Ops:
  0.2 0.8 select_reduce_fusion.10
  1.2 0.6 reduce_max.9
  2.5 0.6 iota.59
  3.6 254.2 %conditional.1 = (f32[1,2,512,512]{3,2,1,0:T(8,128)S(1)}) conditional(s32[]{:T(128)} %clamp.8, (s32[4]{0:T(128)}, s32[]{:T(128)}, f32[1024,512]{1,0:T(8,128)}, s32[2]{0:T(128)S(1)}, (), /*index=5*/s32[]{:T(128)}, s32[]{:T(128)}, s32[]{:T(128)}, s32[16,16]{1,0:T(8,128)S(1)}, s32[]{:T(128)}, /*index=10*/s32[]{:T(128)}, s32[]{:T(128)}, s32[]{:T(128)}, ...), branch_computations={%region_10.11_spmd, %region_11.12_spmd} | conditional | flops 9665780736 | bytes 278945120 | solution.py:303
  3.6 1.8 copy.50
  5.3 31.6 %all_to_all.16 = f32[8,2,64,512]{3,2,1,0:T(8,128)S(1)} all-to-all(f32[8,2,64,512]{3,2,1,0:T(8,128)S(1)} %bitcast.44), channel_id=1, replica_groups=mesh['row'=4,'z'=4,'y'=2] {'y','row'}, dimensions={0} | all-to-all | bytes 4194304 | tf_op jit(solution)/shard_map/cond/branch_0_fun/all_to_all | solution.py:247
  37.2 1.1 copy-done
  38.2 0.6 collective-permute-start.8
  39.0 0.6 collective-permute-start.20
  39.7 1.5 collective-permute-start.10
  41.1 1.5 collective-permute-start.18
  43.2 21.2 %collective-permute-done.8.refs_0_ = f32[2,8,32,512]{3,2,1,0:T(8,128)} collective-permute-done((f32[2,8,32,512]{3,2,1,0:T(8,128)S(1)}, f32[2,8,32,512]{3,2,1,0:T(8,128)}, u32[]{:S(2)}, u32[]{:S(2)}) %collective-permute-start.8) | collective-permute-done | bytes 1048608 | tf_op jit(solution)/shard_map/cond/branch_0_fun/ppermute | solution.py:230
  64.6 0.6 reshape.172.index_ref
  65.2 0.6 collective-permute-start.28
  65.8 0.7 collective-permute-start.30
  66.5 9.1 %branch_0_fun.14 = (f32[12,64,128]{2,1,0:T(8,128)}, f32[12,64,128]{2,1,0:T(8,128)}, f32[12,64,128]{2,1,0:T(8,128)}, f32[12,64,128]{2,1,0:T(8,128)}, f32[12,64,12...) custom-call(s32[2]{0:T(128)S(1)} %get-tuple-element.34.meta_ref, s32[12]{0:T(128)} %constant.67.clone.1.pairs_ref, ...), custom_call_target="tpu_custom_call" | custom-call | flops 2415919104 | bytes 16777216 | tf_op jit(solution)/shard_map/cond/branch_0_fun/pallas_call | solution.py:64
  75.6 12.0 %collective-permute-done.10.refs_2_ = f32[2,8,32,512]{3,2,1,0:T(8,128)} collective-permute-done((f32[2,8,32,512]{3,2,1,0:T(8,128)S(1)}, f32[2,8,32,512]{3,2,1,0:T(8,128)}, u32[]{:S(2)}, u32[]{:S(2)}) %collective-permute-start.10) | collective-permute-done | bytes 1048608 | tf_op jit(solution)/shard_map/cond/branch_0_fun/ppermute | solution.py:232
  87.6 3.5 %collective-permute-start.2 = (f32[12,64,128]{2,1,0:T(8,128)}, f32[12,64,128]{2,1,0:T(8,128)S(1)}, u32[]{:S(2)}, u32[]{:S(2)}) collective-permute-start(f32[12,64,128]{2,1,0:T(8,128)} %get-tuple-element.39), channel_id=1, source_target_pairs={{0,2},{1,3},{8,10},{9,11},{16,18},{17,19},{24,26},{25,27}} | collective-permute-start | bytes 1179656 | tf_op jit(solution)/shard_map/cond/branch_0_fun/ppermute | solution.py:267
  91.1 0.7 collective-permute-start.3
  91.8 6.8 %collective-permute-done.2.up_ref = f32[12,64,128]{2,1,0:T(8,128)S(1)} collective-permute-done((f32[12,64,128]{2,1,0:T(8,128)}, f32[12,64,128]{2,1,0:T(8,128)S(1)}, u32[]{:S(2)}, u32[]{:S(2)}) %collective-permute-start.2) | collective-permute-done | bytes 393248 | tf_op jit(solution)/shard_map/cond/branch_0_fun/ppermute | solution.py:267
  99.3 10.1 %collective-permute-done.28.refs_0_ = f32[2,8,32,512]{3,2,1,0:T(8,128)} collective-permute-done((f32[2,8,32,512]{3,2,1,0:T(8,128)}, f32[2,8,32,512]{3,2,1,0:T(8,128)}, u32[]{:S(2)}, u32[]{:S(2)}) %collective-permute-start.28) | collective-permute-done | bytes 1048608 | tf_op jit(solution)/shard_map/cond/branch_0_fun/ppermute | solution.py:232
  109.9 2.3 branch_0_fun.15
  112.2 3.5 %collective-permute-start.4 = (f32[12,64,128]{2,1,0:T(8,128)}, f32[12,64,128]{2,1,0:T(8,128)S(1)}, u32[]{:S(2)}, u32[]{:S(2)}) collective-permute-start(f32[12,64,128]{2,1,0:T(8,128)} %get-tuple-element.43), channel_id=1, source_target_pairs={{0,2},{2,4},{1,3},{3,5},{8,10},{10,12},{9,11},{11,13},{16,18},{18,... | collective-permute-start | bytes 1179656 | tf_op jit(solution)/shard_map/cond/branch_0_fun/ppermute | solution.py:267
  115.7 9.0 %branch_0_fun.17 = (f32[12,64,128]{2,1,0:T(8,128)}, f32[12,64,128]{2,1,0:T(8,128)}, f32[12,64,128]{2,1,0:T(8,128)}, f32[12,64,128]{2,1,0:T(8,128)}, f32[12,64,12...) custom-call(s32[2]{0:T(128)S(1)} %get-tuple-element.34.meta_ref, s32[12]{0:T(128)} %constant.67.clone.1.pairs_ref, ...), custom_call_target="tpu_custom_call" | custom-call | flops 2415919104 | bytes 16777216 | tf_op jit(solution)/shard_map/cond/branch_0_fun/pallas_call | solution.py:64
  124.7 3.5 %collective-permute-start.12 = (f32[12,64,128]{2,1,0:T(8,128)}, f32[12,64,128]{2,1,0:T(8,128)S(1)}, u32[]{:S(2)}, u32[]{:S(2)}) collective-permute-start(f32[12,64,128]{2,1,0:T(8,128)} %get-tuple-element.50), channel_id=1, source_target_pairs={{0,2},{1,3},{8,10},{9,11},{16,18},{17,19},{24,26},{25,27}} | collective-permute-start | bytes 1179656 | tf_op jit(solution)/shard_map/cond/branch_0_fun/ppermute | solution.py:267
  128.2 0.7 collective-permute-start.13
  128.9 9.1 %branch_0_fun.20 = (f32[12,64,128]{2,1,0:T(8,128)}, f32[12,64,128]{2,1,0:T(8,128)}, f32[12,64,128]{2,1,0:T(8,128)}, f32[12,64,128]{2,1,0:T(8,128)}, f32[12,64,12...) custom-call(s32[2]{0:T(128)S(1)} %get-tuple-element.34.meta_ref, s32[12]{0:T(128)} %constant.67.clone.1.pairs_ref, ...), custom_call_target="tpu_custom_call" | custom-call | flops 2415919104 | bytes 16777216 | tf_op jit(solution)/shard_map/cond/branch_0_fun/pallas_call | solution.py:64
  138.0 1.3 collective-permute-start.22
  139.3 0.8 collective-permute-start.23
  140.2 9.0 %branch_0_fun.23 = (f32[12,64,128]{2,1,0:T(8,128)}, f32[12,64,128]{2,1,0:T(8,128)}, f32[12,64,128]{2,1,0:T(8,128)}, f32[12,64,128]{2,1,0:T(8,128)}, f32[12,64,12...) custom-call(s32[2]{0:T(128)S(1)} %get-tuple-element.34.meta_ref, s32[12]{0:T(128)} %constant.67.clone.1.pairs_ref, ...), custom_call_target="tpu_custom_call" | custom-call | flops 2415919104 | bytes 16777216 | tf_op jit(solution)/shard_map/cond/branch_0_fun/pallas_call | solution.py:64
  149.2 0.7 collective-permute-start.5
  149.9 1.9 collective-permute-start.32
  151.8 1.4 collective-permute-start.33
  153.3 2.3 branch_0_fun.18
  155.5 1.3 collective-permute-start.14
  156.9 0.7 collective-permute-start.15
  157.6 2.3 branch_0_fun.21
  159.9 4.4 %collective-permute-start.24 = (f32[12,64,128]{2,1,0:T(8,128)}, f32[12,64,128]{2,1,0:T(8,128)S(1)}, u32[]{:S(2)}, u32[]{:S(2)}) collective-permute-start(f32[12,64,128]{2,1,0:T(8,128)} %get-tuple-element.65), channel_id=1, source_target_pairs={{0,2},{2,4},{1,3},{3,5},{8,10},{10,12},{9,11},{11,13},{16,18},{18,... | collective-permute-start | bytes 1179656 | tf_op jit(solution)/shard_map/cond/branch_0_fun/ppermute | solution.py:267
  164.3 0.7 collective-permute-start.25
  165.1 2.3 branch_0_fun.16
  167.4 2.3 branch_0_fun.24
  169.7 5.1 %collective-permute-start.34 = (f32[12,64,128]{2,1,0:T(8,128)}, f32[12,64,128]{2,1,0:T(8,128)S(1)}, u32[]{:S(2)}, u32[]{:S(2)}) collective-permute-start(f32[12,64,128]{2,1,0:T(8,128)} %get-tuple-element.76), channel_id=1, source_target_pairs={{0,2},{2,4},{1,3},{3,5},{8,10},{10,12},{9,11},{11,13},{16,18},{18,... | collective-permute-start | bytes 1179656 | tf_op jit(solution)/shard_map/cond/branch_0_fun/ppermute | solution.py:267
  174.9 0.7 collective-permute-start.35
  175.6 5.2 %collective-permute-start.6 = (f32[12,64,128]{2,1,0:T(8,128)}, f32[12,64,128]{2,1,0:T(8,128)S(1)}, u32[]{:S(2)}, u32[]{:S(2)}) collective-permute-start(f32[12,64,128]{2,1,0:T(8,128)} %get-tuple-element.47), channel_id=1, source_target_pairs={{0,2},{2,4},{4,6},{1,3},{3,5},{5,7},{8,10},{10,12},{12,14},{9,11},... | collective-permute-start | bytes 1179656 | tf_op jit(solution)/shard_map/cond/branch_0_fun/ppermute | solution.py:267
  180.8 2.3 branch_0_fun.19
  183.1 1.3 collective-permute-start.7
  184.4 5.2 %collective-permute-start.16 = (f32[12,64,128]{2,1,0:T(8,128)}, f32[12,64,128]{2,1,0:T(8,128)S(1)}, u32[]{:S(2)}, u32[]{:S(2)}) collective-permute-start(f32[12,64,128]{2,1,0:T(8,128)} %get-tuple-element.58), channel_id=1, source_target_pairs={{0,2},{2,4},{4,6},{1,3},{3,5},{5,7},{8,10},{10,12},{12,14},{9,11},... | collective-permute-start | bytes 1179656 | tf_op jit(solution)/shard_map/cond/branch_0_fun/ppermute | solution.py:267
  189.6 2.3 branch_0_fun.22
  191.9 1.3 collective-permute-start.17
  193.2 4.6 %collective-permute-start.26 = (f32[12,64,128]{2,1,0:T(8,128)}, f32[12,64,128]{2,1,0:T(8,128)S(1)}, u32[]{:S(2)}, u32[]{:S(2)}) collective-permute-start(f32[12,64,128]{2,1,0:T(8,128)} %get-tuple-element.69), channel_id=1, source_target_pairs={{0,2},{2,4},{4,6},{1,3},{3,5},{5,7},{8,10},{10,12},{12,14},{9,11},... | collective-permute-start | bytes 1179656 | tf_op jit(solution)/shard_map/cond/branch_0_fun/ppermute | solution.py:267
  197.8 2.3 branch_0_fun.25
  200.2 1.3 collective-permute-start.27
  201.5 4.6 %collective-permute-start.36 = (f32[12,64,128]{2,1,0:T(8,128)}, f32[12,64,128]{2,1,0:T(8,128)S(1)}, u32[]{:S(2)}, u32[]{:S(2)}) collective-permute-start(f32[12,64,128]{2,1,0:T(8,128)} %get-tuple-element.80), channel_id=1, source_target_pairs={{0,2},{2,4},{4,6},{1,3},{3,5},{5,7},{8,10},{10,12},{12,14},{9,11},... | collective-permute-start | bytes 1179656 | tf_op jit(solution)/shard_map/cond/branch_0_fun/ppermute | solution.py:267
  206.1 1.3 collective-permute-start.37
  207.6 0.7 reduce_sum.96.live_ref
  208.3 0.6 broadcast_minimum_fusion.spread_ref
  208.9 3.2 %collective-permute-done.26.refs_7_ = f32[12,64,128]{2,1,0:T(8,128)S(1)} collective-permute-done((f32[12,64,128]{2,1,0:T(8,128)}, f32[12,64,128]{2,1,0:T(8,128)S(1)}, u32[]{:S(2)}, u32[]{:S(2)}) %collective-permute-start.26) | collective-permute-done | bytes 393248 | tf_op jit(solution)/shard_map/cond/branch_0_fun/ppermute | solution.py:267
  212.1 2.1 collective-permute-done.27.refs_8_
  214.3 5.1 %collective-permute-done.36.refs_10_ = f32[12,64,128]{2,1,0:T(8,128)S(1)} collective-permute-done((f32[12,64,128]{2,1,0:T(8,128)}, f32[12,64,128]{2,1,0:T(8,128)S(1)}, u32[]{:S(2)}, u32[]{:S(2)}) %collective-permute-start.36) | collective-permute-done | bytes 393248 | tf_op jit(solution)/shard_map/cond/branch_0_fun/ppermute | solution.py:267
  220.1 0.5 copy-done.33
  220.6 4.0 %branch_0_fun.26 = f32[8,4,2,64,128]{4,3,2,1,0:T(8,128)} custom-call(s32[16]{0:T(128)} %broadcast_minimum_fusion.spread_ref, s32[16]{0:T(128)} %reduce_sum.96.live_ref, f32[12,64,128]{2,1,0:T(8,128)} %get-tuple-element.38.refs_0_, f32[12,64,128]{2,1,0:T(8,128)} %copy-done.26, f32[12,64,128]{2,1,0:T(8,128)} %copy-done.27, ...), custom_call_target="tpu_custom_call" | custom-call | tf_op jit(solution)/shard_map/cond/branch_0_fun/pallas_call | solution.py:111
  224.6 30.9 %all_to_all.17.in_ref = f32[8,4,2,64,128]{4,3,2,1,0:T(8,128)} all-to-all(f32[8,4,2,64,128]{4,3,2,1,0:T(8,128)} %branch_0_fun.26), channel_id=1, replica_groups=mesh['row'=4,'z'=4,'y'=2] {'y','row'}, dimensions={0} | all-to-all | bytes 4194304 | tf_op jit(solution)/shard_map/cond/branch_0_fun/all_to_all | solution.py:285
  255.5 2.0 branch_0_fun.27
  257.8 1.3 copy-done.2
  (128 shorter events, 4.5 us)
Async XLA Ops:
  38.2 28.3 %copy-start.3 = (f32[2,8,32,512]{3,2,1,0:T(8,128)}, f32[2,8,32,512]{3,2,1,0:T(8,128)S(1)}, u32[]{:S(2)}) copy-start(f32[2,8,32,512]{3,2,1,0:T(8,128)S(1)} %get-tuple-element.454.refs_2_) | copy-start | bytes 3145732 | tf_op jit(solution)/shard_map/cond
  38.2 28.3 %copy-start.5 = (f32[2,8,32,512]{3,2,1,0:T(8,128)}, f32[2,8,32,512]{3,2,1,0:T(8,128)S(1)}, u32[]{:S(2)}) copy-start(f32[2,8,32,512]{3,2,1,0:T(8,128)S(1)} %get-tuple-element.455.refs_0_) | copy-start | bytes 3145732 | tf_op jit(solution)/shard_map/cond
  38.2 2.9 %collective-permute-start = (f32[2,8,32,512]{3,2,1,0:T(8,128)S(1)}, f32[2,8,32,512]{3,2,1,0:T(8,128)}, u32[]{:S(2)}, u32[]{:S(2)}) collective-permute-start(f32[2,8,32,512]{3,2,1,0:T(8,128)S(1)} %get-tuple-element.455.refs_0_), channel_id=1, source_target_pairs={{0,8},{8,0},{16,24},{24,16},{1,9},{9,1},{17,25},{25,17},{2,10},{10... | collective-permute-start | bytes 3145736 | tf_op jit(solution)/shard_map/cond/branch_0_fun/ppermute | solution.py:237
  38.2 26.1 %collective-permute-start.8 = (f32[2,8,32,512]{3,2,1,0:T(8,128)S(1)}, f32[2,8,32,512]{3,2,1,0:T(8,128)}, u32[]{:S(2)}, u32[]{:S(2)}) collective-permute-start(f32[2,8,32,512]{3,2,1,0:T(8,128)S(1)} %get-tuple-element.455.refs_0_), channel_id=1, source_target_pairs={{0,16},{8,24},{16,0},{24,8},{1,17},{9,25},{17,1},{25,9},{2,18},{10... | collective-permute-start | bytes 3145736 | tf_op jit(solution)/shard_map/cond/branch_0_fun/ppermute | solution.py:230
  38.8 26.4 %collective-permute-start.1 = (f32[2,8,32,512]{3,2,1,0:T(8,128)S(1)}, f32[2,8,32,512]{3,2,1,0:T(8,128)}, u32[]{:S(2)}, u32[]{:S(2)}) collective-permute-start(f32[2,8,32,512]{3,2,1,0:T(8,128)S(1)} %get-tuple-element.454.refs_2_), channel_id=1, source_target_pairs={{0,8},{8,0},{16,24},{24,16},{1,9},{9,1},{17,25},{25,17},{2,10},{10... | collective-permute-start | bytes 3145736 | tf_op jit(solution)/shard_map/cond/branch_0_fun/ppermute | solution.py:237
  39.0 26.8 %collective-permute-start.20 = (f32[2,8,32,512]{3,2,1,0:T(8,128)S(1)}, f32[2,8,32,512]{3,2,1,0:T(8,128)S(1)}, u32[]{:S(2)}, u32[]{:S(2)}) collective-permute-start(f32[2,8,32,512]{3,2,1,0:T(8,128)S(1)} %get-tuple-element.454.refs_2_), channel_id=1, source_target_pairs={{0,1},{1,0},{2,3},{3,2},{4,5},{5,4},{6,7},{7,6},{8,9},{9,8},{10,11... | collective-permute-start | bytes 3145736 | tf_op jit(solution)/shard_map/cond/branch_0_fun/ppermute | solution.py:232
  39.7 48.0 %collective-permute-start.10 = (f32[2,8,32,512]{3,2,1,0:T(8,128)S(1)}, f32[2,8,32,512]{3,2,1,0:T(8,128)}, u32[]{:S(2)}, u32[]{:S(2)}) collective-permute-start(f32[2,8,32,512]{3,2,1,0:T(8,128)S(1)} %get-tuple-element.455.refs_0_), channel_id=1, source_target_pairs={{0,1},{1,0},{2,3},{3,2},{4,5},{5,4},{6,7},{7,6},{8,9},{9,8},{10,11... | collective-permute-start | bytes 3145736 | tf_op jit(solution)/shard_map/cond/branch_0_fun/ppermute | solution.py:232
  41.1 50.0 %collective-permute-start.18 = (f32[2,8,32,512]{3,2,1,0:T(8,128)S(1)}, f32[2,8,32,512]{3,2,1,0:T(8,128)}, u32[]{:S(2)}, u32[]{:S(2)}) collective-permute-start(f32[2,8,32,512]{3,2,1,0:T(8,128)S(1)} %get-tuple-element.454.refs_2_), channel_id=1, source_target_pairs={{0,16},{8,24},{16,0},{24,8},{1,17},{9,25},{17,1},{25,9},{2,18},{10... | collective-permute-start | bytes 3145736 | tf_op jit(solution)/shard_map/cond/branch_0_fun/ppermute | solution.py:230
  64.4 34.8 %collective-permute-start.9 = (f32[2,8,32,512]{3,2,1,0:T(8,128)}, f32[2,8,32,512]{3,2,1,0:T(8,128)}, u32[]{:S(2)}, u32[]{:S(2)}) collective-permute-start(f32[2,8,32,512]{3,2,1,0:T(8,128)} %collective-permute-done.8.refs_0_), channel_id=1, source_target_pairs={{0,8},{8,0},{16,24},{24,16},{1,9},{9,1},{17,25},{25,17},{2,10},{10... | collective-permute-start | bytes 3145736 | tf_op jit(solution)/shard_map/cond/branch_0_fun/ppermute | solution.py:237
  65.2 44.2 %collective-permute-start.28 = (f32[2,8,32,512]{3,2,1,0:T(8,128)}, f32[2,8,32,512]{3,2,1,0:T(8,128)}, u32[]{:S(2)}, u32[]{:S(2)}) collective-permute-start(f32[2,8,32,512]{3,2,1,0:T(8,128)} %collective-permute-done.8.refs_0_), channel_id=1, source_target_pairs={{0,1},{1,0},{2,3},{3,2},{4,5},{5,4},{6,7},{7,6},{8,9},{9,8},{10,11... | collective-permute-start | bytes 3145736 | tf_op jit(solution)/shard_map/cond/branch_0_fun/ppermute | solution.py:232
  65.8 33.4 %copy-start.51 = (f32[2,8,32,512]{3,2,1,0:T(8,128)}, f32[2,8,32,512]{3,2,1,0:T(8,128)S(1)}, u32[]{:S(2)}) copy-start(f32[2,8,32,512]{3,2,1,0:T(8,128)S(1)} %collective-permute-done.20.refs_2_) | copy-start | bytes 3145732 | tf_op jit(solution)/shard_map/cond
  65.8 43.6 %collective-permute-start.30 = (f32[2,8,32,512]{3,2,1,0:T(8,128)S(1)}, f32[2,8,32,512]{3,2,1,0:T(8,128)}, u32[]{:S(2)}, u32[]{:S(2)}) collective-permute-start(f32[2,8,32,512]{3,2,1,0:T(8,128)S(1)} %collective-permute-done.20.refs_2_), channel_id=1, source_target_pairs={{0,16},{8,24},{16,0},{24,8},{1,17},{9,25},{17,1},{25,9},{2,18},{10... | collective-permute-start | bytes 3145736 | tf_op jit(solution)/shard_map/cond/branch_0_fun/ppermute | solution.py:230
  87.6 11.1 %collective-permute-start.2 = (f32[12,64,128]{2,1,0:T(8,128)}, f32[12,64,128]{2,1,0:T(8,128)S(1)}, u32[]{:S(2)}, u32[]{:S(2)}) collective-permute-start(f32[12,64,128]{2,1,0:T(8,128)} %get-tuple-element.39), channel_id=1, source_target_pairs={{0,2},{1,3},{8,10},{9,11},{16,18},{17,19},{24,26},{25,27}} | collective-permute-start | bytes 1179656 | tf_op jit(solution)/shard_map/cond/branch_0_fun/ppermute | solution.py:267
  91.1 7.5 %collective-permute-start.3 = (f32[12,64,128]{2,1,0:T(8,128)}, f32[12,64,128]{2,1,0:T(8,128)S(1)}, u32[]{:S(2)}, u32[]{:S(2)}) collective-permute-start(f32[12,64,128]{2,1,0:T(8,128)} %get-tuple-element.41), channel_id=1, source_target_pairs={{6,4},{7,5},{14,12},{15,13},{22,20},{23,21},{30,28},{31,29}} | collective-permute-start | bytes 1179656 | tf_op jit(solution)/shard_map/cond/branch_0_fun/ppermute | solution.py:268
  98.7 11.3 %copy-start.47 = (f32[12,64,128]{2,1,0:T(8,128)}, f32[12,64,128]{2,1,0:T(8,128)S(1)}, u32[]{:S(2)}) copy-start(f32[12,64,128]{2,1,0:T(8,128)S(1)} %collective-permute-done.2.up_ref) | copy-start | bytes 1179652 | tf_op jit(solution)/shard_map/cond
  98.7 13.5 %collective-permute-start.11 = (f32[2,8,32,512]{3,2,1,0:T(8,128)}, f32[2,8,32,512]{3,2,1,0:T(8,128)}, u32[]{:S(2)}, u32[]{:S(2)}) collective-permute-start(f32[2,8,32,512]{3,2,1,0:T(8,128)} %collective-permute-done.10.refs_2_), channel_id=1, source_target_pairs={{0,8},{8,0},{16,24},{24,16},{1,9},{9,1},{17,25},{25,17},{2,10},{10... | collective-permute-start | bytes 3145736 | tf_op jit(solution)/shard_map/cond/branch_0_fun/ppermute | solution.py:237
  98.7 11.2 %copy-start.48 = (f32[12,64,128]{2,1,0:T(8,128)}, f32[12,64,128]{2,1,0:T(8,128)S(1)}, u32[]{:S(2)}) copy-start(f32[12,64,128]{2,1,0:T(8,128)S(1)} %collective-permute-done.3.down_ref) | copy-start | bytes 1179652 | tf_op jit(solution)/shard_map/cond
  98.7 26.0 %collective-permute-start.19 = (f32[2,8,32,512]{3,2,1,0:T(8,128)}, f32[2,8,32,512]{3,2,1,0:T(8,128)}, u32[]{:S(2)}, u32[]{:S(2)}) collective-permute-start(f32[2,8,32,512]{3,2,1,0:T(8,128)} %collective-permute-done.18.refs_0_), channel_id=1, source_target_pairs={{0,8},{8,0},{16,24},{24,16},{1,9},{9,1},{17,25},{25,17},{2,10},{10... | collective-permute-start | bytes 3145736 | tf_op jit(solution)/shard_map/cond/branch_0_fun/ppermute | solution.py:237
  99.2 29.0 %collective-permute-start.21 = (f32[2,8,32,512]{3,2,1,0:T(8,128)S(1)}, f32[2,8,32,512]{3,2,1,0:T(8,128)}, u32[]{:S(2)}, u32[]{:S(2)}) collective-permute-start(f32[2,8,32,512]{3,2,1,0:T(8,128)S(1)} %collective-permute-done.20.refs_2_), channel_id=1, source_target_pairs={{0,8},{8,0},{16,24},{24,16},{1,9},{9,1},{17,25},{25,17},{2,10},{10... | collective-permute-start | bytes 3145736 | tf_op jit(solution)/shard_map/cond/branch_0_fun/ppermute | solution.py:237
  109.4 28.6 %collective-permute-start.29 = (f32[2,8,32,512]{3,2,1,0:T(8,128)}, f32[2,8,32,512]{3,2,1,0:T(8,128)}, u32[]{:S(2)}, u32[]{:S(2)}) collective-permute-start(f32[2,8,32,512]{3,2,1,0:T(8,128)} %collective-permute-done.28.refs_0_), channel_id=1, source_target_pairs={{0,8},{8,0},{16,24},{24,16},{1,9},{9,1},{17,25},{25,17},{2,10},{10... | collective-permute-start | bytes 3145736 | tf_op jit(solution)/shard_map/cond/branch_0_fun/ppermute | solution.py:237
  109.4 29.9 %collective-permute-start.31 = (f32[2,8,32,512]{3,2,1,0:T(8,128)}, f32[2,8,32,512]{3,2,1,0:T(8,128)}, u32[]{:S(2)}, u32[]{:S(2)}) collective-permute-start(f32[2,8,32,512]{3,2,1,0:T(8,128)} %collective-permute-done.30.refs_2_), channel_id=1, source_target_pairs={{0,8},{8,0},{16,24},{24,16},{1,9},{9,1},{17,25},{25,17},{2,10},{10... | collective-permute-start | bytes 3145736 | tf_op jit(solution)/shard_map/cond/branch_0_fun/ppermute | solution.py:237
  112.2 37.0 %collective-permute-start.4 = (f32[12,64,128]{2,1,0:T(8,128)}, f32[12,64,128]{2,1,0:T(8,128)S(1)}, u32[]{:S(2)}, u32[]{:S(2)}) collective-permute-start(f32[12,64,128]{2,1,0:T(8,128)} %get-tuple-element.43), channel_id=1, source_target_pairs={{0,2},{2,4},{1,3},{3,5},{8,10},{10,12},{9,11},{11,13},{16,18},{18,... | collective-permute-start | bytes 1179656 | tf_op jit(solution)/shard_map/cond/branch_0_fun/ppermute | solution.py:267
  124.7 25.2 %collective-permute-start.12 = (f32[12,64,128]{2,1,0:T(8,128)}, f32[12,64,128]{2,1,0:T(8,128)S(1)}, u32[]{:S(2)}, u32[]{:S(2)}) collective-permute-start(f32[12,64,128]{2,1,0:T(8,128)} %get-tuple-element.50), channel_id=1, source_target_pairs={{0,2},{1,3},{8,10},{9,11},{16,18},{17,19},{24,26},{25,27}} | collective-permute-start | bytes 1179656 | tf_op jit(solution)/shard_map/cond/branch_0_fun/ppermute | solution.py:267
  128.2 23.6 %collective-permute-start.13 = (f32[12,64,128]{2,1,0:T(8,128)}, f32[12,64,128]{2,1,0:T(8,128)S(1)}, u32[]{:S(2)}, u32[]{:S(2)}) collective-permute-start(f32[12,64,128]{2,1,0:T(8,128)} %get-tuple-element.52), channel_id=1, source_target_pairs={{6,4},{7,5},{14,12},{15,13},{22,20},{23,21},{30,28},{31,29}} | collective-permute-start | bytes 1179656 | tf_op jit(solution)/shard_map/cond/branch_0_fun/ppermute | solution.py:268
  138.0 17.5 %collective-permute-start.22 = (f32[12,64,128]{2,1,0:T(8,128)}, f32[12,64,128]{2,1,0:T(8,128)S(1)}, u32[]{:S(2)}, u32[]{:S(2)}) collective-permute-start(f32[12,64,128]{2,1,0:T(8,128)} %get-tuple-element.61), channel_id=1, source_target_pairs={{0,2},{1,3},{8,10},{9,11},{16,18},{17,19},{24,26},{25,27}} | collective-permute-start | bytes 1179656 | tf_op jit(solution)/shard_map/cond/branch_0_fun/ppermute | solution.py:267
  139.3 9.9 %copy-start.53 = (f32[12,64,128]{2,1,0:T(8,128)S(1)}, f32[12,64,128]{2,1,0:T(8,128)}, u32[]{:S(2)}) copy-start(f32[12,64,128]{2,1,0:T(8,128)} %get-tuple-element.45) | copy-start | bytes 1179652 | tf_op jit(solution)/shard_map/cond
  139.3 17.5 %collective-permute-start.23 = (f32[12,64,128]{2,1,0:T(8,128)}, f32[12,64,128]{2,1,0:T(8,128)S(1)}, u32[]{:S(2)}, u32[]{:S(2)}) collective-permute-start(f32[12,64,128]{2,1,0:T(8,128)} %get-tuple-element.63), channel_id=1, source_target_pairs={{6,4},{7,5},{14,12},{15,13},{22,20},{23,21},{30,28},{31,29}} | collective-permute-start | bytes 1179656 | tf_op jit(solution)/shard_map/cond/branch_0_fun/ppermute | solution.py:268
  149.2 15.9 %copy-start.34 = (f32[12,64,128]{2,1,0:T(8,128)}, f32[12,64,128]{2,1,0:T(8,128)S(1)}, u32[]{:S(2)}) copy-start(f32[12,64,128]{2,1,0:T(8,128)S(1)} %collective-permute-done.4.up_ref) | copy-start | bytes 1179652 | tf_op jit(solution)/shard_map/cond
  149.2 10.7 %collective-permute-start.5 = (f32[12,64,128]{2,1,0:T(8,128)S(1)}, f32[12,64,128]{2,1,0:T(8,128)S(1)}, u32[]{:S(2)}, u32[]{:S(2)}) collective-permute-start(f32[12,64,128]{2,1,0:T(8,128)S(1)} %copy-done.53), channel_id=1, source_target_pairs={{6,4},{4,2},{7,5},{5,3},{14,12},{12,10},{15,13},{13,11},{22,20},{2... | collective-permute-start | bytes 1179656 | tf_op jit(solution)/shard_map/cond/branch_0_fun/ppermute | solution.py:268
  149.9 3.3 %copy-start.35 = (f32[12,64,128]{2,1,0:T(8,128)}, f32[12,64,128]{2,1,0:T(8,128)S(1)}, u32[]{:S(2)}) copy-start(f32[12,64,128]{2,1,0:T(8,128)S(1)} %collective-permute-done.12.up_ref) | copy-start | bytes 1179652 | tf_op jit(solution)/shard_map/cond
  149.9 14.4 %collective-permute-start.32 = (f32[12,64,128]{2,1,0:T(8,128)}, f32[12,64,128]{2,1,0:T(8,128)S(1)}, u32[]{:S(2)}, u32[]{:S(2)}) collective-permute-start(f32[12,64,128]{2,1,0:T(8,128)} %get-tuple-element.72), channel_id=1, source_target_pairs={{0,2},{1,3},{8,10},{9,11},{16,18},{17,19},{24,26},{25,27}} | collective-permute-start | bytes 1179656 | tf_op jit(solution)/shard_map/cond/branch_0_fun/ppermute | solution.py:267
  151.8 1.4 copy-start.39
  151.8 15.5 %collective-permute-start.33 = (f32[12,64,128]{2,1,0:T(8,128)}, f32[12,64,128]{2,1,0:T(8,128)}, u32[]{:S(2)}, u32[]{:S(2)}) collective-permute-start(f32[12,64,128]{2,1,0:T(8,128)} %get-tuple-element.74), channel_id=1, source_target_pairs={{6,4},{7,5},{14,12},{15,13},{22,20},{23,21},{30,28},{31,29}} | collective-permute-start | bytes 1179656 | tf_op jit(solution)/shard_map/cond/branch_0_fun/ppermute | solution.py:268
  155.5 2.0 copy-start.38
  155.5 19.3 %collective-permute-start.14 = (f32[12,64,128]{2,1,0:T(8,128)}, f32[12,64,128]{2,1,0:T(8,128)S(1)}, u32[]{:S(2)}, u32[]{:S(2)}) collective-permute-start(f32[12,64,128]{2,1,0:T(8,128)} %get-tuple-element.54), channel_id=1, source_target_pairs={{0,2},{2,4},{1,3},{3,5},{8,10},{10,12},{9,11},{11,13},{16,18},{18,... | collective-permute-start | bytes 1179656 | tf_op jit(solution)/shard_map/cond/branch_0_fun/ppermute | solution.py:267
  156.9 18.7 %collective-permute-start.15 = (f32[12,64,128]{2,1,0:T(8,128)}, f32[12,64,128]{2,1,0:T(8,128)S(1)}, u32[]{:S(2)}, u32[]{:S(2)}) collective-permute-start(f32[12,64,128]{2,1,0:T(8,128)} %get-tuple-element.56), channel_id=1, source_target_pairs={{6,4},{4,2},{7,5},{5,3},{14,12},{12,10},{15,13},{13,11},{22,20},{2... | collective-permute-start | bytes 1179656 | tf_op jit(solution)/shard_map/cond/branch_0_fun/ppermute | solution.py:268
  159.9 5.1 %copy-start.43 = (f32[12,64,128]{2,1,0:T(8,128)}, f32[12,64,128]{2,1,0:T(8,128)S(1)}, u32[]{:S(2)}) copy-start(f32[12,64,128]{2,1,0:T(8,128)S(1)} %collective-permute-done.5.down_ref) | copy-start | bytes 1179652 | tf_op jit(solution)/shard_map/cond
  159.9 23.1 %collective-permute-start.24 = (f32[12,64,128]{2,1,0:T(8,128)}, f32[12,64,128]{2,1,0:T(8,128)S(1)}, u32[]{:S(2)}, u32[]{:S(2)}) collective-permute-start(f32[12,64,128]{2,1,0:T(8,128)} %get-tuple-element.65), channel_id=1, source_target_pairs={{0,2},{2,4},{1,3},{3,5},{8,10},{10,12},{9,11},{11,13},{16,18},{18,... | collective-permute-start | bytes 1179656 | tf_op jit(solution)/shard_map/cond/branch_0_fun/ppermute | solution.py:267
  164.3 3.0 %copy-start.40 = (f32[12,64,128]{2,1,0:T(8,128)}, f32[12,64,128]{2,1,0:T(8,128)S(1)}, u32[]{:S(2)}) copy-start(f32[12,64,128]{2,1,0:T(8,128)S(1)} %collective-permute-done.32.up_ref) | copy-start | bytes 1179652 | tf_op jit(solution)/shard_map/cond
  164.3 20.0 %collective-permute-start.25 = (f32[12,64,128]{2,1,0:T(8,128)}, f32[12,64,128]{2,1,0:T(8,128)S(1)}, u32[]{:S(2)}, u32[]{:S(2)}) collective-permute-start(f32[12,64,128]{2,1,0:T(8,128)} %get-tuple-element.67), channel_id=1, source_target_pairs={{6,4},{4,2},{7,5},{5,3},{14,12},{12,10},{15,13},{13,11},{22,20},{2... | collective-permute-start | bytes 1179656 | tf_op jit(solution)/shard_map/cond/branch_0_fun/ppermute | solution.py:268
  165.1 24.5 %copy-start.54 = (s32[4]{0:T(128)S(1)}, s32[4]{0:T(128)}, u32[]{:S(2)}) copy-start(s32[4]{0:T(128)} %get-tuple-element.423) | copy-start | bytes 52 | tf_op jit(solution)/shard_map/cond
  169.7 22.2 %collective-permute-start.34 = (f32[12,64,128]{2,1,0:T(8,128)}, f32[12,64,128]{2,1,0:T(8,128)S(1)}, u32[]{:S(2)}, u32[]{:S(2)}) collective-permute-start(f32[12,64,128]{2,1,0:T(8,128)} %get-tuple-element.76), channel_id=1, source_target_pairs={{0,2},{2,4},{1,3},{3,5},{8,10},{10,12},{9,11},{11,13},{16,18},{18,... | collective-permute-start | bytes 1179656 | tf_op jit(solution)/shard_map/cond/branch_0_fun/ppermute | solution.py:267
  174.9 5.9 %copy-start.37 = (f32[12,64,128]{2,1,0:T(8,128)}, f32[12,64,128]{2,1,0:T(8,128)S(1)}, u32[]{:S(2)}) copy-start(f32[12,64,128]{2,1,0:T(8,128)S(1)} %collective-permute-done.14.up_ref) | copy-start | bytes 1179652 | tf_op jit(solution)/shard_map/cond
  174.9 18.3 %collective-permute-start.35 = (f32[12,64,128]{2,1,0:T(8,128)}, f32[12,64,128]{2,1,0:T(8,128)S(1)}, u32[]{:S(2)}, u32[]{:S(2)}) collective-permute-start(f32[12,64,128]{2,1,0:T(8,128)} %get-tuple-element.78), channel_id=1, source_target_pairs={{6,4},{4,2},{7,5},{5,3},{14,12},{12,10},{15,13},{13,11},{22,20},{2... | collective-permute-start | bytes 1179656 | tf_op jit(solution)/shard_map/cond/branch_0_fun/ppermute | solution.py:268
  175.6 5.2 %copy-start.45 = (f32[12,64,128]{2,1,0:T(8,128)}, f32[12,64,128]{2,1,0:T(8,128)S(1)}, u32[]{:S(2)}) copy-start(f32[12,64,128]{2,1,0:T(8,128)S(1)} %collective-permute-done.15.down_ref) | copy-start | bytes 1179652 | tf_op jit(solution)/shard_map/cond
  175.6 24.6 %collective-permute-start.6 = (f32[12,64,128]{2,1,0:T(8,128)}, f32[12,64,128]{2,1,0:T(8,128)S(1)}, u32[]{:S(2)}, u32[]{:S(2)}) collective-permute-start(f32[12,64,128]{2,1,0:T(8,128)} %get-tuple-element.47), channel_id=1, source_target_pairs={{0,2},{2,4},{4,6},{1,3},{3,5},{5,7},{8,10},{10,12},{12,14},{9,11},... | collective-permute-start | bytes 1179656 | tf_op jit(solution)/shard_map/cond/branch_0_fun/ppermute | solution.py:267
  183.1 6.5 %copy-start.36 = (f32[12,64,128]{2,1,0:T(8,128)}, f32[12,64,128]{2,1,0:T(8,128)S(1)}, u32[]{:S(2)}) copy-start(f32[12,64,128]{2,1,0:T(8,128)S(1)} %collective-permute-done.24.up_ref) | copy-start | bytes 1179652 | tf_op jit(solution)/shard_map/cond
  183.1 18.4 %collective-permute-start.7 = (f32[12,64,128]{2,1,0:T(8,128)}, f32[12,64,128]{2,1,0:T(8,128)S(1)}, u32[]{:S(2)}, u32[]{:S(2)}) collective-permute-start(f32[12,64,128]{2,1,0:T(8,128)} %get-tuple-element.48), channel_id=1, source_target_pairs={{6,4},{4,2},{2,0},{7,5},{5,3},{3,1},{14,12},{12,10},{10,8},{15,13}... | collective-permute-start | bytes 1179656 | tf_op jit(solution)/shard_map/cond/branch_0_fun/ppermute | solution.py:268
  184.4 5.2 %copy-start.44 = (f32[12,64,128]{2,1,0:T(8,128)}, f32[12,64,128]{2,1,0:T(8,128)S(1)}, u32[]{:S(2)}) copy-start(f32[12,64,128]{2,1,0:T(8,128)S(1)} %collective-permute-done.25.down_ref) | copy-start | bytes 1179652 | tf_op jit(solution)/shard_map/cond
  184.4 21.7 %collective-permute-start.16 = (f32[12,64,128]{2,1,0:T(8,128)}, f32[12,64,128]{2,1,0:T(8,128)S(1)}, u32[]{:S(2)}, u32[]{:S(2)}) collective-permute-start(f32[12,64,128]{2,1,0:T(8,128)} %get-tuple-element.58), channel_id=1, source_target_pairs={{0,2},{2,4},{4,6},{1,3},{3,5},{5,7},{8,10},{10,12},{12,14},{9,11},... | collective-permute-start | bytes 1179656 | tf_op jit(solution)/shard_map/cond/branch_0_fun/ppermute | solution.py:267
  191.9 5.9 %copy-start.41 = (f32[12,64,128]{2,1,0:T(8,128)}, f32[12,64,128]{2,1,0:T(8,128)S(1)}, u32[]{:S(2)}) copy-start(f32[12,64,128]{2,1,0:T(8,128)S(1)} %collective-permute-done.34.up_ref) | copy-start | bytes 1179652 | tf_op jit(solution)/shard_map/cond
  191.9 17.0 %collective-permute-start.17 = (f32[12,64,128]{2,1,0:T(8,128)}, f32[12,64,128]{2,1,0:T(8,128)S(1)}, u32[]{:S(2)}, u32[]{:S(2)}) collective-permute-start(f32[12,64,128]{2,1,0:T(8,128)} %get-tuple-element.59), channel_id=1, source_target_pairs={{6,4},{4,2},{2,0},{7,5},{5,3},{3,1},{14,12},{12,10},{10,8},{15,13}... | collective-permute-start | bytes 1179656 | tf_op jit(solution)/shard_map/cond/branch_0_fun/ppermute | solution.py:268
  193.2 4.6 %copy-start.46 = (f32[12,64,128]{2,1,0:T(8,128)}, f32[12,64,128]{2,1,0:T(8,128)S(1)}, u32[]{:S(2)}) copy-start(f32[12,64,128]{2,1,0:T(8,128)S(1)} %collective-permute-done.35.down_ref) | copy-start | bytes 1179652 | tf_op jit(solution)/shard_map/cond
  193.2 18.9 %collective-permute-start.26 = (f32[12,64,128]{2,1,0:T(8,128)}, f32[12,64,128]{2,1,0:T(8,128)S(1)}, u32[]{:S(2)}, u32[]{:S(2)}) collective-permute-start(f32[12,64,128]{2,1,0:T(8,128)} %get-tuple-element.69), channel_id=1, source_target_pairs={{0,2},{2,4},{4,6},{1,3},{3,5},{5,7},{8,10},{10,12},{12,14},{9,11},... | collective-permute-start | bytes 1179656 | tf_op jit(solution)/shard_map/cond/branch_0_fun/ppermute | solution.py:267
  200.2 19.7 %copy-start.26 = (f32[12,64,128]{2,1,0:T(8,128)}, f32[12,64,128]{2,1,0:T(8,128)S(1)}, u32[]{:S(2)}) copy-start(f32[12,64,128]{2,1,0:T(8,128)S(1)} %collective-permute-done.6.refs_1_) | copy-start | bytes 1179652 | tf_op jit(solution)/shard_map/cond
  200.2 14.1 %collective-permute-start.27 = (f32[12,64,128]{2,1,0:T(8,128)}, f32[12,64,128]{2,1,0:T(8,128)S(1)}, u32[]{:S(2)}, u32[]{:S(2)}) collective-permute-start(f32[12,64,128]{2,1,0:T(8,128)} %get-tuple-element.70), channel_id=1, source_target_pairs={{6,4},{4,2},{2,0},{7,5},{5,3},{3,1},{14,12},{12,10},{10,8},{15,13}... | collective-permute-start | bytes 1179656 | tf_op jit(solution)/shard_map/cond/branch_0_fun/ppermute | solution.py:268
  201.5 18.4 %copy-start.27 = (f32[12,64,128]{2,1,0:T(8,128)}, f32[12,64,128]{2,1,0:T(8,128)S(1)}, u32[]{:S(2)}) copy-start(f32[12,64,128]{2,1,0:T(8,128)S(1)} %collective-permute-done.7.refs_2_) | copy-start | bytes 1179652 | tf_op jit(solution)/shard_map/cond
  201.5 17.8 %collective-permute-start.36 = (f32[12,64,128]{2,1,0:T(8,128)}, f32[12,64,128]{2,1,0:T(8,128)S(1)}, u32[]{:S(2)}, u32[]{:S(2)}) collective-permute-start(f32[12,64,128]{2,1,0:T(8,128)} %get-tuple-element.80), channel_id=1, source_target_pairs={{0,2},{2,4},{4,6},{1,3},{3,5},{5,7},{8,10},{10,12},{12,14},{9,11},... | collective-permute-start | bytes 1179656 | tf_op jit(solution)/shard_map/cond/branch_0_fun/ppermute | solution.py:267
  206.1 13.8 %copy-start.28 = (f32[12,64,128]{2,1,0:T(8,128)}, f32[12,64,128]{2,1,0:T(8,128)S(1)}, u32[]{:S(2)}) copy-start(f32[12,64,128]{2,1,0:T(8,128)S(1)} %collective-permute-done.16.refs_4_) | copy-start | bytes 1179652 | tf_op jit(solution)/shard_map/cond
  206.1 13.8 %collective-permute-start.37 = (f32[12,64,128]{2,1,0:T(8,128)}, f32[12,64,128]{2,1,0:T(8,128)S(1)}, u32[]{:S(2)}, u32[]{:S(2)}) collective-permute-start(f32[12,64,128]{2,1,0:T(8,128)} %get-tuple-element.81), channel_id=1, source_target_pairs={{6,4},{4,2},{2,0},{7,5},{5,3},{3,1},{14,12},{12,10},{10,8},{15,13}... | collective-permute-start | bytes 1179656 | tf_op jit(solution)/shard_map/cond/branch_0_fun/ppermute | solution.py:268
  208.9 11.0 %copy-start.29 = (f32[12,64,128]{2,1,0:T(8,128)}, f32[12,64,128]{2,1,0:T(8,128)S(1)}, u32[]{:S(2)}) copy-start(f32[12,64,128]{2,1,0:T(8,128)S(1)} %collective-permute-done.17.refs_5_) | copy-start | bytes 1179652 | tf_op jit(solution)/shard_map/cond
  212.1 7.7 %copy-start.30 = (f32[12,64,128]{2,1,0:T(8,128)}, f32[12,64,128]{2,1,0:T(8,128)S(1)}, u32[]{:S(2)}) copy-start(f32[12,64,128]{2,1,0:T(8,128)S(1)} %collective-permute-done.26.refs_7_) | copy-start | bytes 1179652 | tf_op jit(solution)/shard_map/cond
  214.3 5.6 %copy-start.31 = (f32[12,64,128]{2,1,0:T(8,128)}, f32[12,64,128]{2,1,0:T(8,128)S(1)}, u32[]{:S(2)}) copy-start(f32[12,64,128]{2,1,0:T(8,128)S(1)} %collective-permute-done.27.refs_8_) | copy-start | bytes 1179652 | tf_op jit(solution)/shard_map/cond
  257.8 1.3 copy-start.2
  (4 other events, 3.6 us)

commit v2 on v1

v2 whole, which is shorter than its diff:
```python
import functools

import jax
import jax.numpy as jnp
from jax import lax
from jax.experimental import pallas as pl
from jax.experimental.pallas import tpu as pltpu
from jax.sharding import Mesh, PartitionSpec as P

BLOCK = 512
WIDE = 256


def split_hi_lo(x):
    hi = x.astype(jnp.bfloat16)
    lo = (x - hi.astype(jnp.float32)).astype(jnp.bfloat16)
    return hi, lo


def product_kernel(dims, outs, meta_ref, pairs_ref, index_ref, s_ref, *refs):
    blocks, h, kc, ys, rb, cb, n_pairs = dims
    pieces, lists, (s_cat, j_cat, part) = refs[:4], refs[4 : 4 + outs], refs[4 + outs :]
    core = meta_ref[0]
    q = h // 2

    def put(target, row, y, x, right):
        hi, lo = split_hi_lo(x)
        base = 3 * kc * y
        rows = pl.ds(pl.multiple_of(row, q), x.shape[0])
        target[rows, base : base + kc] = hi
        target[rows, base + kc : base + 2 * kc] = lo if right else hi
        target[rows, base + 2 * kc : base + 3 * kc] = hi if right else lo

    @pl.loop(0, blocks)
    def _(j):
        for y in range(ys):
            put(s_cat, j * h, y, s_ref[y, j], False)
            for at, piece in enumerate(pieces):
                side = core if at % 2 == 0 else 1 - core
                put(j_cat, j * 2 * h + (at // 2 * 2 + side) * q, y, piece[y, j], True)

    @pl.loop(0, n_pairs)
    def _(t):
        ib, jb = pairs_ref[2 * t], pairs_ref[2 * t + 1]
        left = s_cat[pl.ds(pl.multiple_of(ib * rb, rb), rb), :]
        right = j_cat[pl.ds(pl.multiple_of(jb * cb, cb), cb), :]
        out = lax.dot_general(left, right, (((1,), (1,)), ((), ())), preferred_element_type=jnp.float32)
        for a in range(rb // h):
            for b in range(cb // (2 * h)):
                where = (ib * (rb // h) + a) * blocks + jb * (cb // (2 * h)) + b
                part[where] = out[a * h : (a + 1) * h, b * 2 * h : (b + 1) * 2 * h]

    base = 0
    for one in lists:

        @pl.loop(0, one.shape[0])
        def _(k, one=one, base=base):
            one[k] = part[index_ref[base + k]]

        base += one.shape[0]


def products(dims, sizes, meta, pairs, index, s, pieces):
    blocks, h, kc, ys, rb, cb, n_pairs = dims
    outs = len(sizes)
    k3 = 3 * kc * ys
    smem, vmem = pl.BlockSpec(memory_space=pltpu.SMEM), pl.BlockSpec(memory_space=pltpu.VMEM)
    flops = 2 * n_pairs * rb * cb * k3
    return pl.pallas_call(
        functools.partial(product_kernel, dims, outs),
        out_shape=[jax.ShapeDtypeStruct((size, h, 2 * h), jnp.float32) for size in sizes],
        in_specs=[smem] * 3 + [vmem] * 5,
        out_specs=[vmem] * outs,
        scratch_shapes=[
            pltpu.VMEM((blocks * h, k3), jnp.bfloat16),
            pltpu.VMEM((blocks * 2 * h, k3), jnp.bfloat16),
            pltpu.VMEM((blocks * blocks, h, 2 * h), jnp.float32),
        ],
        cost_estimate=pl.CostEstimate(flops=flops, bytes_accessed=8 * s.size * 4, transcendentals=0),
    )(meta, pairs, index, s, *pieces)


def pick_kernel(chunks, spread_ref, live_ref, *refs):
    out_ref = refs[-1]
    devices, _, slots = out_ref.shape[:3]
    entries = devices * slots
    each = (len(refs) - 1) // chunks

    @pl.loop(0, devices)
    def _(d):
        for slot in range(slots):
            e = d * slots + slot
            used = live_ref[e] > 0
            for c in range(chunks):
                total = refs[each * c][e]
                for step in range(1, each):
                    total += refs[each * c + step][spread_ref[(step - 1) * entries + e]]
                out_ref[d, c, slot] = jnp.where(used, total, jnp.zeros_like(total))


def pick(plane, slots, chunks, spread, live, terms):
    smem, vmem = pl.BlockSpec(memory_space=pltpu.SMEM), pl.BlockSpec(memory_space=pltpu.VMEM)
    shape = (plane, chunks, slots) + terms[0].shape[1:]
    return pl.pallas_call(
        functools.partial(pick_kernel, chunks),
        out_shape=jax.ShapeDtypeStruct(shape, jnp.float32),
        in_specs=[smem] * 2 + [vmem] * len(terms),
        out_specs=vmem,
    )(spread, live, *terms)


def place_kernel(plan, *refs):
    in_refs, out_ref = refs[:-1], refs[-1]
    h, w = in_refs[0].shape[3:]
    q = h // 2
    for source, chip, side, parts in plan:
        for col, spots in parts:
            cols = slice(col * w, (col + 1) * w)
            first, second = spots[0][0], spots[1][0]
            for half in range(2):
                row = chip * w + half * h + side * q
                rows = slice(half * q, (half + 1) * q)
                if first == second:
                    out_ref[:, row : row + q, cols] = in_refs[first[0]][source, first[1], :, rows, :]
                else:
                    halves = []
                    for (group, at), spot in spots:
                        halves.append(in_refs[group][source, at, :, rows, spot * h : (spot + 1) * h])
                    out_ref[:, row : row + q, cols] = jnp.concatenate(halves, axis=2)


def place(plan, arrived):
    vmem = pl.BlockSpec(memory_space=pltpu.VMEM)
    return pl.pallas_call(
        functools.partial(place_kernel, plan),
        out_shape=jax.ShapeDtypeStruct((arrived[0].shape[2], BLOCK, BLOCK), jnp.float32),
        in_specs=[vmem] * len(arrived),
        out_specs=vmem,
    )(*arrived)


def list_tables(owner_slot, rows_n, zs, ys, slots, per_group):
    blocks = owner_slot.shape[0]
    positions = zs * ys * slots
    block_row = jnp.arange(blocks, dtype=jnp.int32)[:, None]
    block_col = jnp.arange(blocks, dtype=jnp.int32)[None, :]
    inside = block_col <= block_row
    wanted = jnp.arange(positions, dtype=jnp.int32)
    matched = (inside[None] & (owner_slot[None] == wanted[:, None, None])).reshape(positions, rows_n, per_group, blocks)
    tile_id = (block_row * blocks + block_col).reshape(1, rows_n, per_group, blocks)
    tile = jnp.sum(jnp.where(matched, tile_id, 0), axis=(2, 3))
    live = jnp.sum(matched.astype(jnp.int32), axis=(2, 3))
    entries = ys * rows_n * slots

    def by_plane(x):
        return x.reshape(zs, ys, slots, rows_n).transpose(0, 1, 3, 2).reshape(zs, entries)

    tile, live = by_plane(tile), by_plane(live)
    order = jnp.arange(entries, dtype=jnp.int32)
    before = order[None, :, None] > order[None, None, :]
    rank = jnp.sum(jnp.where(before, live[:, None, :], 0), axis=2)
    count = jnp.sum(live, axis=1)
    return tile, live, rank, count


def make_plan(chips, zs):
    singles = [u for u in range(1, chips) if u & (u - 1) == 0]
    chunks = [((0, 0), (0, 1))]
    if len(singles) > 1:
        chunks += [((singles[-1], half), (singles[0], half)) for half in range(2)]
    used = {u for chunk in chunks for u, _ in chunk}
    chunks += [((u, 0), (u, 1)) for u in range(1, chips) if u not in used]
    gap = 2 if len(chunks) <= 4 else 2 * zs
    events = []
    for c in range(len(chunks)):
        events.append((gap * c, "product", c, 0))
        events.extend((gap * c + 2 * step - 1.8 + 0.01 * step, "step", c, step) for step in range(2, zs))
        if c:
            events.append((gap * c - 0.5, "fetch", c, 0))
    groups = [list(range(c, min(c + 2, len(chunks)))) for c in range(0, len(chunks), 2)]
    events.extend((gap * group[-1] + 2 * zs - 1.7, "early", at, 0) for at, group in enumerate(groups[:-1]))
    events.sort(key=lambda e: e[0])
    return chunks, events, groups


def link_of(u, half):
    return u & -u if half == 0 else 1 << (u.bit_length() - 1)


def body(panel_rows, owner_slot):
    rows_n, zs, ys = (lax.axis_size(name) for name in ("row", "z", "y"))
    slab_rows, kc = panel_rows.shape
    per_group = slab_rows // BLOCK
    blocks = per_group * rows_n
    cols_n = zs * ys
    row_tiles = per_group * (blocks - per_group) + per_group * (per_group + 1) // 2
    slots = (row_tiles + cols_n - 1) // cols_n
    plane = rows_n * ys
    chips = plane // 2
    h = BLOCK // plane
    rb, cb = min(WIDE, blocks * h), min(2 * WIDE, blocks * 2 * h)
    per_i, per_j = rb // h, cb // (2 * h)
    pair_list = [
        (ib, jb)
        for ib in range(blocks // per_i)
        for jb in range(blocks // per_j)
        if ib * per_i + per_i - 1 >= jb * per_j
    ]
    dims = (blocks, h, kc, ys, rb, cb, len(pair_list))
    pairs = jnp.array([v for pair in pair_list for v in pair], jnp.int32)
    my_z, my_row, my_y = (lax.axis_index(name) for name in ("z", "row", "y"))
    meta = jnp.stack([my_row % 2, (my_row // 2) * ys + my_y]).astype(jnp.int32)
    sliced = panel_rows.reshape(per_group, rows_n // 2, ys, 2, 2, h // 2, kc).transpose(2, 1, 4, 0, 3, 5, 6)
    sliced = sliced.reshape(plane, per_group, h, kc)
    s = lax.all_to_all(sliced, ("y", "row"), 0, 0, tiled=True).reshape(ys, blocks, h, kc)
    tile, live, rank, count = list_tables(owner_slot, rows_n, zs, ys, slots, per_group)
    entries = ys * rows_n * slots
    tiles = blocks * (blocks + 1) // 2

    planes = jnp.arange(zs, dtype=jnp.int32)
    above = jnp.sum(jnp.where(planes[None, :] > planes[:, None], count[None, :], 0), axis=1)
    below = jnp.sum(jnp.where(planes[None, :] < planes[:, None], count[None, :], 0), axis=1)
    up_at, down_at = above[:, None] + rank, below[:, None] + rank
    places = jnp.arange(tiles, dtype=jnp.int32)

    def in_order(at):
        hit = (at[None] == places[:, None, None]) & (live[None] > 0)
        return jnp.sum(jnp.where(hit, tile[None], 0), axis=(1, 2))

    up_order, down_order = in_order(up_at), in_order(down_at)
    own = (planes == my_z)[:, None]
    my_tile, my_live, my_up, my_down = (jnp.sum(jnp.where(own, t, 0), axis=0) for t in (tile, live, up_at, down_at))
    index = jnp.stack([jnp.where(my_z == step - 1, up_order, down_order) for step in range(1, zs)])
    spread = jnp.stack(
        [jnp.where(my_z == step, my_up, jnp.where(my_z == zs - 1 - step, my_down, 0)) for step in range(1, zs)]
    )
    needed = [jnp.maximum(above[step - 1], below[zs - step]) for step in range(1, zs)]

    def chip_swap(x, u):
        ux, uy = u // ys, u % ys
        if uy == 0:
            return lax.ppermute(x, "row", [(r, r ^ (2 * ux)) for r in range(rows_n)])
        if ux == 0:
            return lax.ppermute(x, "y", [(y, y ^ uy) for y in range(ys)])
        perm = [(r * ys + y, (r ^ (2 * ux)) * ys + (y ^ uy)) for r in range(rows_n) for y in range(ys)]
        return lax.ppermute(x, ("row", "y"), perm)

    def core_swap(x):
        return lax.ppermute(x, "row", [(r, r ^ 1) for r in range(rows_n)])

    chunks, events, groups = make_plan(chips, zs)

    def run(sizes, *args):
        return run_scoped(sizes, *args)

    def run_scoped(sizes, s, index, spread, my_tile, my_live):
        same, peer = {(0, 0): s[:, :, : h // 2], (0, 1): s[:, :, h // 2 :]}, {}

        def cores(u, half):
            peer[u, half] = core_swap(same[u, half])

        def reach(u, half):
            if (u, half) not in same:
                low = link_of(u, half)
                reach(u ^ low, half)
                same[u, half] = chip_swap(same[u ^ low, half], low)

        for half in range(2):
            cores(0, half)
            for u in range(1, chips):
                reach(u, half)
        flat_index = jnp.concatenate([index[i, :size] for i, size in enumerate(sizes)] + [my_tile])
        limit = jnp.array(sizes, jnp.int32)[:, None] - 1
        flat_spread = jnp.minimum(spread, limit).reshape(-1)
        lists, flows, arrived = {}, {}, []

        def forward(c, step, x):
            flows[c, step] = lax.ppermute(x, "z", [(step - 1, step), (zs - step, zs - step - 1)])

        def deliver(group):
            terms = [x for c in group for x in (lists[c][-1], *(flows[c, step] for step in range(1, zs)))]
            ready = pick(plane, slots, len(group), flat_spread, my_live, terms)
            arrived.append(lax.all_to_all(ready, ("y", "row"), 0, 0, tiled=True))

        for _, kind, c, step in events:
            if kind == "fetch":
                for u, half in chunks[c]:
                    cores(u, half)
            elif kind == "product":
                pieces = [side[key] for key in chunks[c] for side in (same, peer)]
                lists[c] = products(dims, (*sizes, entries), meta, pairs, flat_index, s, pieces)
                forward(c, 1, lists[c][0])
            elif kind == "step":
                own = lists[c][step - 1]
                passed = flows[c, step - 1][: own.shape[0]] + own
                forward(c, step, passed)
            else:
                deliver(groups[c])

        deliver(groups[-1])
        plan = []
        for d in range(plane):
            chip = (d % rows_n) // 2 * ys + d // rows_n
            parts = []
            for u in range(chips):
                spots = []
                for half in range(2):
                    c = next(i for i, chunk in enumerate(chunks) if (u, half) in chunk)
                    where = next((g, group.index(c)) for g, group in enumerate(groups) if c in group)
                    spots.append((where, chunks[c].index((u, half))))
                parts.append((chip ^ u, tuple(spots)))
            plan.append((d, chip, d % 2, tuple(parts)))
        return place(tuple(plan), arrived)[None]

    mean = [-(-tiles * (zs - step) // zs) for step in range(1, zs)]
    whole = tuple(min(tiles, (zs - step) * entries) for step in range(1, zs))
    sizes = [tuple(min(m + extra, w) for m, w, extra in zip(mean, whole, (low, *[low + 1] * zs))) for low in (1, 3)]
    which = 0
    for choice in sizes:
        fits = functools.reduce(jnp.logical_and, [need <= size for need, size in zip(needed, choice)])
        which += 1 - fits.astype(jnp.int32)
    sizes.append(whole)
    branches = [functools.partial(run, size) for size in sizes]
    return lax.switch(which, branches, s, index, spread, my_tile, my_live)


def solution(mesh):
    rows_n, cols_n = mesh.shape["row"], mesh.shape["col"]
    ys = 2 if cols_n % 2 == 0 else 1
    fine = Mesh(mesh.devices.reshape(rows_n, cols_n // ys, ys), ("row", "z", "y"))
    return jax.shard_map(
        body,
        mesh=fine,
        in_specs=(P("row", ("z", "y")), P()),
        out_specs=P("row", ("z", "y"), None, None),
        check_vma=False,
    )
```

time: 264 us -> 243 us (0.920); the launches traced: 259 us -> 242 us
  waiting for transfers between devices: 61.2 us -> 119 us
  blocking collectives: 62.4 us -> 19.6 us
  starting transfers between devices: 62.2 us -> 36.6 us
  Pallas kernels: 60.6 us -> 42.4 us
  other arithmetic: 3.07 us -> 12.7 us
  between operations: 0.69 us -> 3.79 us
    all_to_all x2 -> x1, blocking collectives: 62.4 us -> 19.6 us  [deliver(): arrived.append(lax.all_to_all(ready, ('y', 'row'), 0, 0, tiled=True))]
    ppermute x24 -> x12, starting transfers between devices: 55.4 us -> 20.8 us  [forward(): lax.ppermute(x, 'z', [(step - 1, step), (zs - step, zs - step - 1)])]
    ppermute x24 -> x12, waiting for transfers between devices: 17.8 us -> 45.2 us  [forward(): lax.ppermute(x, 'z', [(step - 1, step), (zs - step, zs - step - 1)])]
    all_to_all x0 -> x2, waiting for transfers between devices: none -> 20 us  [the longest x1 20 us: body(): lax.all_to_all(sliced, ('y', 'row'), 0, 0, tiled=True)]
    pallas_call x9 -> x2, Pallas kernels: 22.4 us -> 7.17 us  [pick(): pl.pallas_call(functools.partial(pick_kernel, chunks), out_shape=jax.Shap...]
    add x0 -> x8, other arithmetic: none -> 10.9 us  [run_scoped(): passed = flows[c, step - 1][:own.shape[0]] + own]
    all_to_all x0 -> x2, starting transfers between devices: none -> 8.89 us  [the longest x1 5.33 us: body(): lax.all_to_all(sliced, ('y', 'row'), 0, 0, tiled=True)]
    ppermute x3, waiting for transfers between devices: 22.2 us -> 29.7 us  [chip_swap(): return lax.ppermute(x, 'y', [(y, y ^ uy) for y in range(ys)])]
  transfers between devices with their start and end apart: 38 -> 28, of which waited for: 8 -> 10; matrix products, arithmetic and copies ran while one was open for 1% -> 6% of each run, Pallas kernels for 21% -> 16%
where the time goes in v2:
time: 243 us; the launch traced here: 242 us
  waiting for transfers between devices  119 us (49%)
  Pallas kernels  42.4 us (17%)
  starting transfers between devices  36.6 us (15%)
  blocking collectives  19.6 us (8%)
  other arithmetic  12.7 us (5%)
  local copies, waits for them, and re-layouts  7.21 us (3%)
  between operations  3.79 us (2%)
    ppermute x12, waiting for transfers between devices, forward(): lax.ppermute(x, 'z', [(step - 1, step), (zs - step, zs - step - 1)])  45.2 us
    pallas_call x4, Pallas kernels, products(): pl.pallas_call(functools.partial(product_kernel, dims, outs), out_shape=[...  32 us
    ppermute x3, waiting for transfers between devices, chip_swap(): return lax.ppermute(x, 'y', [(y, y ^ uy) for y in range(ys)])  29.7 us
    ppermute x3, waiting for transfers between devices, chip_swap(): return lax.ppermute(x, 'row', [(r, r ^ 2 * ux) for r in range(rows_n)])  24.3 us
    ppermute x12, starting transfers between devices, forward(): lax.ppermute(x, 'z', [(step - 1, step), (zs - step, zs - step - 1)])  20.8 us
    all_to_all x1, waiting for transfers between devices, body(): lax.all_to_all(sliced, ('y', 'row'), 0, 0, tiled=True)  20 us
    all_to_all x1, blocking collectives, deliver(): arrived.append(lax.all_to_all(ready, ('y', 'row'), 0, 0, tiled=True))  19.6 us
    add x8, other arithmetic, run_scoped(): passed = flows[c, step - 1][:own.shape[0]] + own  10.9 us
  transfers between devices with their start and end apart: 28, of which 10 were waited for; matrix products, arithmetic and copies ran while one was open for 6% of the time, Pallas kernels for 16%

profile of v2, /device:TPU:0, one launch (start us, length us, event | category | flops | bytes accessed | tf_op | source)
XLA Modules:
  0.0 241.8 jit_solution(2729928913483883891)
XLA Ops:
  0.0 3.2 %copy.47 = f32[2,2,2,2,2,32,512]{6,5,4,3,2,1,0:T(8,128)} copy(f32[2,2,2,2,2,32,512]{6,5,2,4,0,1,3:T(8,128)} %bitcast.52) | data formatting | bytes 4194304 | tf_op jit(solution)/shard_map/transpose | solution.py:213
  3.2 5.3 %all-to-all-start.6 = ((f32[8,2,64,512]{3,2,1,0:T(8,128)}), f32[8,2,64,512]{3,2,1,0:T(8,128)S(1)}, u32[]{:S(2)}, u32[]{:S(2)}) async-start(f32[8,2,64,512]{3,2,1,0:T(8,128)} %bitcast.51), calls=%async_computation.6 | async-start | bytes 4194304 | tf_op jit(solution)/shard_map/all_to_all | solution.py:215
  8.7 0.1 select_reduce_fusion.2
  8.9 0.2 reduce_sum.121
  9.1 0.2 select_reduce_fusion.8
  9.2 0.7 fusion.12
  13.7 0.1 copy.40
  14.0 0.1 copy.44
  14.3 0.1 copy.46
  14.5 0.1 copy.48
  14.7 0.2 select_reduce_fusion.3
  14.9 0.1 select_reduce_fusion.6
  15.0 0.1 select_reduce_fusion
  15.1 20.0 %all-to-all-done.6 = f32[8,2,64,512]{3,2,1,0:T(8,128)S(1)} async-done(((f32[8,2,64,512]{3,2,1,0:T(8,128)}), f32[8,2,64,512]{3,2,1,0:T(8,128)S(1)}, u32[]{:S(2)}, u32[]{:S(2)}) %all-to-all-start.6) | async-done | bytes 2097184 | tf_op jit(solution)/shard_map/all_to_all | solution.py:215
  35.1 206.6 %conditional.1 = (f32[1,2,512,512]{3,2,1,0:T(8,128)}) conditional(s32[]{:T(128)} %bitcast.12, ((), s32[3,16]{1,0:T(4,128)S(1)}, s32[1,36]{1,0:T(1,128)S(1)}, s32[1,36]{1,0:T(1,128)S(1)}, s32[1,36]{1,0:T(1,128)S(1)}, /*index=5*/s32[16]{0:T(128)S(1)}, f32[2,8,64,512]{3,2,1,0:T(8,128)S(1)}, s32[2]{0:T(128)S(1)}, s32[6]{0:T(128)S(1)}, ...), branch_computations={%region_13.14_spmd, %region_14.15_spmd, %region_15.16_spmd} | conditional | flops 9665249280 | bytes 264770656 | solution.py:324
  35.1 0.2 fusion.9
  35.4 0.6 collective-permute-start.5
  36.0 0.7 collective-permute-start.7
  36.7 1.4 collective-permute-start.14
  38.1 1.5 collective-permute-start.12
  39.6 22.1 %collective-permute-done.5.refs_0_ = f32[2,8,32,512]{3,2,1,0:T(8,128)} collective-permute-done((f32[2,8,32,512]{3,2,1,0:T(8,128)S(1)}, f32[2,8,32,512]{3,2,1,0:T(8,128)}, u32[]{:S(2)}, u32[]{:S(2)}) %collective-permute-start.5) | collective-permute-done | bytes 1048608 | tf_op jit(solution)/shard_map/cond/branch_0_fun/ppermute | solution.py:242
  61.6 0.5 collective-permute-done.7.refs_2_
  62.2 0.7 collective-permute-start.19
  62.9 21.7 %collective-permute-done.14.refs_2_ = f32[2,8,32,512]{3,2,1,0:T(8,128)} collective-permute-done((f32[2,8,32,512]{3,2,1,0:T(8,128)S(1)}, f32[2,8,32,512]{3,2,1,0:T(8,128)}, u32[]{:S(2)}, u32[]{:S(2)}) %collective-permute-start.14) | collective-permute-done | bytes 1048608 | tf_op jit(solution)/shard_map/cond/branch_0_fun/ppermute | solution.py:244
  84.6 1.5 collective-permute-start.21
  86.3 0.5 collective-permute-start.13
  86.7 0.6 pad_add_fusion.index_ref
  87.4 8.0 %branch_0_fun.7 = (f32[28,64,128]{2,1,0:T(8,128)}, f32[20,64,128]{2,1,0:T(8,128)}, f32[11,64,128]{2,1,0:T(8,128)}, f32[16,64,128]{2,1,0:T(8,128)}) custom-call(s32[2]{0:T(128)S(1)} %get-tuple-element.78.meta_ref, s32[6]{0:T(128)S(1)} %get-tuple-element.79.pairs_ref, s32[75]{0:T(128)} %pad_add_fusion.index_ref, ...), custom_call_target="tpu_custom_call" | custom-call | flops 2415919104 | bytes 16777216 | tf_op jit(solution)/shard_map/cond/branch_0_fun/pallas_call | solution.py:69
  95.3 3.5 %collective-permute-start.2 = (f32[28,64,128]{2,1,0:T(8,128)}, f32[28,64,128]{2,1,0:T(8,128)S(1)}, u32[]{:S(2)}, u32[]{:S(2)}) collective-permute-start(f32[28,64,128]{2,1,0:T(8,128)} %get-tuple-element.86), channel_id=1, source_target_pairs={{0,2},{6,4},{1,3},{7,5},{8,10},{14,12},{9,11},{15,13},{16,18},{22,... | collective-permute-start | bytes 2752520 | tf_op jit(solution)/shard_map/cond/branch_0_fun/ppermute | solution.py:278
  98.9 7.4 %collective-permute-done.19.refs_0_ = f32[2,8,32,512]{3,2,1,0:T(8,128)} collective-permute-done((f32[2,8,32,512]{3,2,1,0:T(8,128)}, f32[2,8,32,512]{3,2,1,0:T(8,128)}, u32[]{:S(2)}, u32[]{:S(2)}) %collective-permute-start.19) | collective-permute-done | bytes 1048608 | tf_op jit(solution)/shard_map/cond/branch_0_fun/ppermute | solution.py:244
  106.3 2.2 collective-permute-done.21.refs_2_
  108.5 8.0 %branch_0_fun.8 = (f32[28,64,128]{2,1,0:T(8,128)}, f32[20,64,128]{2,1,0:T(8,128)}, f32[11,64,128]{2,1,0:T(8,128)}, f32[16,64,128]{2,1,0:T(8,128)}) custom-call(s32[2]{0:T(128)S(1)} %get-tuple-element.78.meta_ref, s32[6]{0:T(128)S(1)} %get-tuple-element.79.pairs_ref, s32[75]{0:T(128)} %pad_add_fusion.index_ref, ...), custom_call_target="tpu_custom_call" | custom-call | flops 2415919104 | bytes 16777216 | tf_op jit(solution)/shard_map/cond/branch_0_fun/pallas_call | solution.py:69
  116.4 4.4 %collective-permute-start.9 = (f32[28,64,128]{2,1,0:T(8,128)}, f32[28,64,128]{2,1,0:T(8,128)}, u32[]{:S(2)}, u32[]{:S(2)}) collective-permute-start(f32[28,64,128]{2,1,0:T(8,128)} %get-tuple-element.90), channel_id=1, source_target_pairs={{0,2},{6,4},{1,3},{7,5},{8,10},{14,12},{9,11},{15,13},{16,18},{22,... | collective-permute-start | bytes 2752520 | tf_op jit(solution)/shard_map/cond/branch_0_fun/ppermute | solution.py:278
  120.9 8.0 %branch_0_fun.10 = (f32[28,64,128]{2,1,0:T(8,128)}, f32[20,64,128]{2,1,0:T(8,128)}, f32[11,64,128]{2,1,0:T(8,128)}, f32[16,64,128]{2,1,0:T(8,128)}) custom-call(s32[2]{0:T(128)S(1)} %get-tuple-element.78.meta_ref, s32[6]{0:T(128)S(1)} %get-tuple-element.79.pairs_ref, s32[75]{0:T(128)} %pad_add_fusion.index_ref, ...), custom_call_target="tpu_custom_call" | custom-call | flops 2415919104 | bytes 16777216 | tf_op jit(solution)/shard_map/cond/branch_0_fun/pallas_call | solution.py:69
  128.9 2.2 collective-permute-start.16
  131.1 2.4 slice_add_fusion.3
  133.4 1.5 collective-permute-start.3
  134.9 8.0 %branch_0_fun.11 = (f32[28,64,128]{2,1,0:T(8,128)}, f32[20,64,128]{2,1,0:T(8,128)}, f32[11,64,128]{2,1,0:T(8,128)}, f32[16,64,128]{2,1,0:T(8,128)}) custom-call(s32[2]{0:T(128)S(1)} %get-tuple-element.78.meta_ref, s32[6]{0:T(128)S(1)} %get-tuple-element.79.pairs_ref, s32[75]{0:T(128)} %pad_add_fusion.index_ref, ...), custom_call_target="tpu_custom_call" | custom-call | flops 2415919104 | bytes 16777216 | tf_op jit(solution)/shard_map/cond/branch_0_fun/pallas_call | solution.py:69
  143.0 1.6 collective-permute-start.23
  144.6 1.4 slice_add_fusion.2
  146.1 0.7 collective-permute-start.10
  146.8 1.8 slice_add_fusion.7
  148.6 1.4 collective-permute-start.4
  150.0 10.6 %collective-permute-done.16.refs_1_ = f32[28,64,128]{2,1,0:T(8,128)} collective-permute-done((f32[28,64,128]{2,1,0:T(8,128)}, f32[28,64,128]{2,1,0:T(8,128)}, u32[]{:S(2)}, u32[]{:S(2)}) %collective-permute-start.16) | collective-permute-done | bytes 917536 | tf_op jit(solution)/shard_map/cond/branch_0_fun/ppermute | solution.py:278
  160.6 2.1 slice_add_fusion.1
  162.7 0.7 collective-permute-start.17
  163.5 0.8 slice_add_fusion.6
  164.3 1.4 collective-permute-start.11
  165.7 14.1 %collective-permute-done.23.refs_5_ = f32[28,64,128]{2,1,0:T(8,128)S(1)} collective-permute-done((f32[28,64,128]{2,1,0:T(8,128)}, f32[28,64,128]{2,1,0:T(8,128)S(1)}, u32[]{:S(2)}, u32[]{:S(2)}) %collective-permute-start.23) | collective-permute-done | bytes 917536 | tf_op jit(solution)/shard_map/cond/branch_0_fun/ppermute | solution.py:278
  179.8 1.0 slice_add_fusion
  180.9 0.7 collective-permute-start.24
  181.7 0.6 reshape.246.spread_ref
  182.3 0.7 copy-done.46
  183.0 3.6 %branch_0_fun.9 = f32[8,2,2,64,128]{4,3,2,1,0:T(8,128)} custom-call(s32[48]{0:T(128)} %reshape.246.spread_ref, s32[16]{0:T(128)S(1)} %get-tuple-element.77.live_ref, f32[16,64,128]{2,1,0:T(8,128)} %get-tuple-element.85.refs_0_, f32[28,64,128]{2,1,0:T(8,128)} %copy-done.8, f32[20,64,128]{2,1,0:T(8,128)} %collective-permute-done.3.refs_2_, ...), custom_call_target="tpu_custom_call" | custom-call | tf_op jit(solution)/shard_map/cond/branch_0_fun/pallas_call | solution.py:104
  186.6 3.6 %all-to-all-start = ((f32[8,2,2,64,128]{4,3,2,1,0:T(8,128)}), f32[8,2,2,64,128]{4,3,2,1,0:T(8,128)S(1)}, u32[]{:S(2)}, u32[]{:S(2)}) async-start(f32[8,2,2,64,128]{4,3,2,1,0:T(8,128)} %branch_0_fun.9), calls=%async_computation | async-start | bytes 2097152 | tf_op jit(solution)/shard_map/cond/branch_0_fun/all_to_all | solution.py:283
  190.2 1.3 slice_add_fusion.5
  191.5 1.3 collective-permute-start.18
  192.8 1.3 collective-permute-start.25
  194.1 13.0 %collective-permute-done.18.refs_3_ = f32[11,64,128]{2,1,0:T(8,128)S(1)} collective-permute-done((f32[11,64,128]{2,1,0:T(8,128)S(1)}, f32[11,64,128]{2,1,0:T(8,128)S(1)}, u32[]{:S(2)}, u32[]{:S(2)}) %collective-permute-start.18) | collective-permute-done | bytes 360480 | tf_op jit(solution)/shard_map/cond/branch_0_fun/ppermute | solution.py:278
  207.2 7.4 %collective-permute-done.25.refs_7_ = f32[11,64,128]{2,1,0:T(8,128)S(1)} collective-permute-done((f32[11,64,128]{2,1,0:T(8,128)S(1)}, f32[11,64,128]{2,1,0:T(8,128)S(1)}, u32[]{:S(2)}, u32[]{:S(2)}) %collective-permute-start.25) | collective-permute-done | bytes 360480 | tf_op jit(solution)/shard_map/cond/branch_0_fun/ppermute | solution.py:278
  214.6 0.7 copy-done.48
  215.3 3.6 %branch_0_fun.12 = f32[8,2,2,64,128]{4,3,2,1,0:T(8,128)} custom-call(s32[48]{0:T(128)} %reshape.246.spread_ref, s32[16]{0:T(128)S(1)} %get-tuple-element.77.live_ref, f32[16,64,128]{2,1,0:T(8,128)} %get-tuple-element.93.refs_0_, f32[28,64,128]{2,1,0:T(8,128)} %collective-permute-done.16.refs_1_, f32[20,64,128]{2,1,0:T(8,128)} %copy-done.15, ...), custom_call_target="tpu_custom_call" | custom-call | tf_op jit(solution)/shard_map/cond/branch_0_fun/pallas_call | solution.py:104
  218.9 19.6 %all_to_all.29.refs_1_ = f32[8,2,2,64,128]{4,3,2,1,0:T(8,128)} all-to-all(f32[8,2,2,64,128]{4,3,2,1,0:T(8,128)} %branch_0_fun.12), channel_id=1, replica_groups=mesh['row'=4,'z'=4,'y'=2] {'y','row'}, dimensions={0} | all-to-all | bytes 2097152 | tf_op jit(solution)/shard_map/cond/branch_0_fun/all_to_all | solution.py:283
  238.5 3.3 %branch_0_fun.13 = f32[2,512,512]{2,1,0:T(8,128)} custom-call(f32[8,2,2,64,128]{4,3,2,1,0:T(8,128)} %copy-done.3, f32[8,2,2,64,128]{4,3,2,1,0:T(8,128)} %all_to_all.29.refs_1_), custom_call_target="tpu_custom_call" | custom-call | tf_op jit(solution)/shard_map/cond/branch_0_fun/pallas_call | solution.py:134
  (91 shorter events, 1.4 us)
Async XLA Ops:
  3.2 5.5 %copy-start.51 = (s32[8,8]{1,0:T(8,128)S(1)}, s32[8,8]{1,0:T(8,128)}, u32[]{:S(2)}) copy-start(s32[8,8]{1,0:T(8,128)} %param.10) | copy-start | bytes 772
  3.2 31.9 %copy-start.63 = (s32[6]{0:T(128)S(1)}, s32[6]{0:T(128)}, u32[]{:S(2)}) copy-start(s32[6]{0:T(128)} %constant.79.clone) | copy-start | bytes 76
  3.2 31.9 %all-to-all-start.6 = ((f32[8,2,64,512]{3,2,1,0:T(8,128)}), f32[8,2,64,512]{3,2,1,0:T(8,128)S(1)}, u32[]{:S(2)}, u32[]{:S(2)}) async-start(f32[8,2,64,512]{3,2,1,0:T(8,128)} %bitcast.51), calls=%async_computation.6 | async-start | bytes 4194304 | tf_op jit(solution)/shard_map/all_to_all | solution.py:215
  35.3 50.8 %copy-start.21 = (f32[2,8,32,512]{3,2,1,0:T(8,128)}, f32[2,8,32,512]{3,2,1,0:T(8,128)S(1)}, u32[]{:S(2)}) copy-start(f32[2,8,32,512]{3,2,1,0:T(8,128)S(1)} %get-tuple-element.176.refs_0_) | copy-start | bytes 3145732 | tf_op jit(solution)/shard_map/cond
  35.4 52.0 %copy-start.20 = (f32[2,8,32,512]{3,2,1,0:T(8,128)}, f32[2,8,32,512]{3,2,1,0:T(8,128)S(1)}, u32[]{:S(2)}) copy-start(f32[2,8,32,512]{3,2,1,0:T(8,128)S(1)} %get-tuple-element.175.refs_2_) | copy-start | bytes 3145732 | tf_op jit(solution)/shard_map/cond
  35.4 2.7 %collective-permute-start = (f32[2,8,32,512]{3,2,1,0:T(8,128)S(1)}, f32[2,8,32,512]{3,2,1,0:T(8,128)S(1)}, u32[]{:S(2)}, u32[]{:S(2)}) collective-permute-start(f32[2,8,32,512]{3,2,1,0:T(8,128)S(1)} %get-tuple-element.176.refs_0_), channel_id=1, source_target_pairs={{0,8},{8,0},{16,24},{24,16},{1,9},{9,1},{17,25},{25,17},{2,10},{10... | collective-permute-start | bytes 3145736 | tf_op jit(solution)/shard_map/cond/branch_0_fun/ppermute | solution.py:249
  35.4 26.2 %collective-permute-start.5 = (f32[2,8,32,512]{3,2,1,0:T(8,128)S(1)}, f32[2,8,32,512]{3,2,1,0:T(8,128)}, u32[]{:S(2)}, u32[]{:S(2)}) collective-permute-start(f32[2,8,32,512]{3,2,1,0:T(8,128)S(1)} %get-tuple-element.176.refs_0_), channel_id=1, source_target_pairs={{0,16},{8,24},{16,0},{24,8},{1,17},{9,25},{17,1},{25,9},{2,18},{10... | collective-permute-start | bytes 3145736 | tf_op jit(solution)/shard_map/cond/branch_0_fun/ppermute | solution.py:242
  36.0 26.1 %collective-permute-start.7 = (f32[2,8,32,512]{3,2,1,0:T(8,128)S(1)}, f32[2,8,32,512]{3,2,1,0:T(8,128)}, u32[]{:S(2)}, u32[]{:S(2)}) collective-permute-start(f32[2,8,32,512]{3,2,1,0:T(8,128)S(1)} %get-tuple-element.176.refs_0_), channel_id=1, source_target_pairs={{0,1},{1,0},{2,3},{3,2},{4,5},{5,4},{6,7},{7,6},{8,9},{9,8},{10,11... | collective-permute-start | bytes 3145736 | tf_op jit(solution)/shard_map/cond/branch_0_fun/ppermute | solution.py:244
  36.7 25.5 %collective-permute-start.1 = (f32[2,8,32,512]{3,2,1,0:T(8,128)S(1)}, f32[2,8,32,512]{3,2,1,0:T(8,128)S(1)}, u32[]{:S(2)}, u32[]{:S(2)}) collective-permute-start(f32[2,8,32,512]{3,2,1,0:T(8,128)S(1)} %get-tuple-element.175.refs_2_), channel_id=1, source_target_pairs={{0,8},{8,0},{16,24},{24,16},{1,9},{9,1},{17,25},{25,17},{2,10},{10... | collective-permute-start | bytes 3145736 | tf_op jit(solution)/shard_map/cond/branch_0_fun/ppermute | solution.py:249
  36.7 48.0 %collective-permute-start.14 = (f32[2,8,32,512]{3,2,1,0:T(8,128)S(1)}, f32[2,8,32,512]{3,2,1,0:T(8,128)}, u32[]{:S(2)}, u32[]{:S(2)}) collective-permute-start(f32[2,8,32,512]{3,2,1,0:T(8,128)S(1)} %get-tuple-element.175.refs_2_), channel_id=1, source_target_pairs={{0,1},{1,0},{2,3},{3,2},{4,5},{5,4},{6,7},{7,6},{8,9},{9,8},{10,11... | collective-permute-start | bytes 3145736 | tf_op jit(solution)/shard_map/cond/branch_0_fun/ppermute | solution.py:244
  38.1 48.1 %copy-start.55 = (f32[2,8,32,512]{3,2,1,0:T(8,128)}, f32[2,8,32,512]{3,2,1,0:T(8,128)S(1)}, u32[]{:S(2)}) copy-start(f32[2,8,32,512]{3,2,1,0:T(8,128)S(1)} %collective-permute-done.refs_1_) | copy-start | bytes 3145732 | tf_op jit(solution)/shard_map/cond
  38.1 48.1 %collective-permute-start.12 = (f32[2,8,32,512]{3,2,1,0:T(8,128)S(1)}, f32[2,8,32,512]{3,2,1,0:T(8,128)}, u32[]{:S(2)}, u32[]{:S(2)}) collective-permute-start(f32[2,8,32,512]{3,2,1,0:T(8,128)S(1)} %get-tuple-element.175.refs_2_), channel_id=1, source_target_pairs={{0,16},{8,24},{16,0},{24,8},{1,17},{9,25},{17,1},{25,9},{2,18},{10... | collective-permute-start | bytes 3145736 | tf_op jit(solution)/shard_map/cond/branch_0_fun/ppermute | solution.py:242
  61.6 24.6 %collective-permute-start.6 = (f32[2,8,32,512]{3,2,1,0:T(8,128)}, f32[2,8,32,512]{3,2,1,0:T(8,128)S(1)}, u32[]{:S(2)}, u32[]{:S(2)}) collective-permute-start(f32[2,8,32,512]{3,2,1,0:T(8,128)} %collective-permute-done.5.refs_0_), channel_id=1, source_target_pairs={{0,8},{8,0},{16,24},{24,16},{1,9},{9,1},{17,25},{25,17},{2,10},{10... | collective-permute-start | bytes 3145736 | tf_op jit(solution)/shard_map/cond/branch_0_fun/ppermute | solution.py:249
  62.2 33.2 %collective-permute-start.8 = (f32[2,8,32,512]{3,2,1,0:T(8,128)}, f32[2,8,32,512]{3,2,1,0:T(8,128)}, u32[]{:S(2)}, u32[]{:S(2)}) collective-permute-start(f32[2,8,32,512]{3,2,1,0:T(8,128)} %collective-permute-done.7.refs_2_), channel_id=1, source_target_pairs={{0,8},{8,0},{16,24},{24,16},{1,9},{9,1},{17,25},{25,17},{2,10},{10... | collective-permute-start | bytes 3145736 | tf_op jit(solution)/shard_map/cond/branch_0_fun/ppermute | solution.py:249
  62.2 25.2 %copy-start.59 = (f32[2,8,32,512]{3,2,1,0:T(8,128)}, f32[2,8,32,512]{3,2,1,0:T(8,128)S(1)}, u32[]{:S(2)}) copy-start(f32[2,8,32,512]{3,2,1,0:T(8,128)S(1)} %collective-permute-done.1.refs_3_) | copy-start | bytes 3145732 | tf_op jit(solution)/shard_map/cond
  62.2 44.1 %collective-permute-start.19 = (f32[2,8,32,512]{3,2,1,0:T(8,128)}, f32[2,8,32,512]{3,2,1,0:T(8,128)}, u32[]{:S(2)}, u32[]{:S(2)}) collective-permute-start(f32[2,8,32,512]{3,2,1,0:T(8,128)} %collective-permute-done.5.refs_0_), channel_id=1, source_target_pairs={{0,1},{1,0},{2,3},{3,2},{4,5},{5,4},{6,7},{7,6},{8,9},{9,8},{10,11... | collective-permute-start | bytes 3145736 | tf_op jit(solution)/shard_map/cond/branch_0_fun/ppermute | solution.py:244
  84.6 23.9 %collective-permute-start.21 = (f32[2,8,32,512]{3,2,1,0:T(8,128)}, f32[2,8,32,512]{3,2,1,0:T(8,128)}, u32[]{:S(2)}, u32[]{:S(2)}) collective-permute-start(f32[2,8,32,512]{3,2,1,0:T(8,128)} %collective-permute-done.14.refs_2_), channel_id=1, source_target_pairs={{0,16},{8,24},{16,0},{24,8},{1,17},{9,25},{17,1},{25,9},{2,18},{10... | collective-permute-start | bytes 3145736 | tf_op jit(solution)/shard_map/cond/branch_0_fun/ppermute | solution.py:242
  86.2 34.7 %collective-permute-start.15 = (f32[2,8,32,512]{3,2,1,0:T(8,128)}, f32[2,8,32,512]{3,2,1,0:T(8,128)}, u32[]{:S(2)}, u32[]{:S(2)}) collective-permute-start(f32[2,8,32,512]{3,2,1,0:T(8,128)} %collective-permute-done.14.refs_2_), channel_id=1, source_target_pairs={{0,8},{8,0},{16,24},{24,16},{1,9},{9,1},{17,25},{25,17},{2,10},{10... | collective-permute-start | bytes 3145736 | tf_op jit(solution)/shard_map/cond/branch_0_fun/ppermute | solution.py:249
  86.3 1.1 copy-start.57
  86.3 30.2 %collective-permute-start.13 = (f32[2,8,32,512]{3,2,1,0:T(8,128)}, f32[2,8,32,512]{3,2,1,0:T(8,128)}, u32[]{:S(2)}, u32[]{:S(2)}) collective-permute-start(f32[2,8,32,512]{3,2,1,0:T(8,128)} %collective-permute-done.12.refs_0_), channel_id=1, source_target_pairs={{0,8},{8,0},{16,24},{24,16},{1,9},{9,1},{17,25},{25,17},{2,10},{10... | collective-permute-start | bytes 3145736 | tf_op jit(solution)/shard_map/cond/branch_0_fun/ppermute | solution.py:249
  95.3 35.7 %collective-permute-start.2 = (f32[28,64,128]{2,1,0:T(8,128)}, f32[28,64,128]{2,1,0:T(8,128)S(1)}, u32[]{:S(2)}, u32[]{:S(2)}) collective-permute-start(f32[28,64,128]{2,1,0:T(8,128)} %get-tuple-element.86), channel_id=1, source_target_pairs={{0,2},{6,4},{1,3},{7,5},{8,10},{14,12},{9,11},{15,13},{16,18},{22,... | collective-permute-start | bytes 2752520 | tf_op jit(solution)/shard_map/cond/branch_0_fun/ppermute | solution.py:278
  106.3 28.7 %collective-permute-start.20 = (f32[2,8,32,512]{3,2,1,0:T(8,128)}, f32[2,8,32,512]{3,2,1,0:T(8,128)}, u32[]{:S(2)}, u32[]{:S(2)}) collective-permute-start(f32[2,8,32,512]{3,2,1,0:T(8,128)} %collective-permute-done.19.refs_0_), channel_id=1, source_target_pairs={{0,8},{8,0},{16,24},{24,16},{1,9},{9,1},{17,25},{25,17},{2,10},{10... | collective-permute-start | bytes 3145736 | tf_op jit(solution)/shard_map/cond/branch_0_fun/ppermute | solution.py:249
  108.5 26.5 %collective-permute-start.22 = (f32[2,8,32,512]{3,2,1,0:T(8,128)}, f32[2,8,32,512]{3,2,1,0:T(8,128)}, u32[]{:S(2)}, u32[]{:S(2)}) collective-permute-start(f32[2,8,32,512]{3,2,1,0:T(8,128)} %collective-permute-done.21.refs_2_), channel_id=1, source_target_pairs={{0,8},{8,0},{16,24},{24,16},{1,9},{9,1},{17,25},{25,17},{2,10},{10... | collective-permute-start | bytes 3145736 | tf_op jit(solution)/shard_map/cond/branch_0_fun/ppermute | solution.py:249
  116.4 28.2 %collective-permute-start.9 = (f32[28,64,128]{2,1,0:T(8,128)}, f32[28,64,128]{2,1,0:T(8,128)}, u32[]{:S(2)}, u32[]{:S(2)}) collective-permute-start(f32[28,64,128]{2,1,0:T(8,128)} %get-tuple-element.90), channel_id=1, source_target_pairs={{0,2},{6,4},{1,3},{7,5},{8,10},{14,12},{9,11},{15,13},{16,18},{22,... | collective-permute-start | bytes 2752520 | tf_op jit(solution)/shard_map/cond/branch_0_fun/ppermute | solution.py:278
  128.9 31.8 %collective-permute-start.16 = (f32[28,64,128]{2,1,0:T(8,128)}, f32[28,64,128]{2,1,0:T(8,128)}, u32[]{:S(2)}, u32[]{:S(2)}) collective-permute-start(f32[28,64,128]{2,1,0:T(8,128)} %get-tuple-element.94), channel_id=1, source_target_pairs={{0,2},{6,4},{1,3},{7,5},{8,10},{14,12},{9,11},{15,13},{16,18},{22,... | collective-permute-start | bytes 2752520 | tf_op jit(solution)/shard_map/cond/branch_0_fun/ppermute | solution.py:278
  131.1 11.9 %copy-start.8 = (f32[28,64,128]{2,1,0:T(8,128)}, f32[28,64,128]{2,1,0:T(8,128)S(1)}, u32[]{:S(2)}) copy-start(f32[28,64,128]{2,1,0:T(8,128)S(1)} %collective-permute-done.2.refs_1_) | copy-start | bytes 2752516 | tf_op jit(solution)/shard_map/cond
  133.4 13.4 %collective-permute-start.3 = (f32[20,64,128]{2,1,0:T(8,128)}, f32[20,64,128]{2,1,0:T(8,128)}, u32[]{:S(2)}, u32[]{:S(2)}) collective-permute-start(f32[20,64,128]{2,1,0:T(8,128)} %slice_add_fusion.3), channel_id=1, source_target_pairs={{2,4},{4,2},{3,5},{5,3},{10,12},{12,10},{11,13},{13,11},{18,20},{2... | collective-permute-start | bytes 1966088 | tf_op jit(solution)/shard_map/cond/branch_0_fun/ppermute | solution.py:278
  143.0 3.8 %copy-start.43 = (f32[11,64,128]{2,1,0:T(8,128)S(1)}, f32[11,64,128]{2,1,0:T(8,128)}, u32[]{:S(2)}) copy-start(f32[11,64,128]{2,1,0:T(8,128)} %get-tuple-element.88) | copy-start | bytes 1081348 | tf_op jit(solution)/shard_map/cond
  143.0 36.8 %collective-permute-start.23 = (f32[28,64,128]{2,1,0:T(8,128)}, f32[28,64,128]{2,1,0:T(8,128)S(1)}, u32[]{:S(2)}, u32[]{:S(2)}) collective-permute-start(f32[28,64,128]{2,1,0:T(8,128)} %get-tuple-element.98), channel_id=1, source_target_pairs={{0,2},{6,4},{1,3},{7,5},{8,10},{14,12},{9,11},{15,13},{16,18},{22,... | collective-permute-start | bytes 2752520 | tf_op jit(solution)/shard_map/cond/branch_0_fun/ppermute | solution.py:278
  144.6 16.0 %copy-start.28 = (f32[20,64,128]{2,1,0:T(8,128)S(1)}, f32[20,64,128]{2,1,0:T(8,128)}, u32[]{:S(2)}) copy-start(f32[20,64,128]{2,1,0:T(8,128)} %get-tuple-element.95) | copy-start | bytes 1966084 | tf_op jit(solution)/shard_map/cond
  146.1 17.4 %collective-permute-start.10 = (f32[20,64,128]{2,1,0:T(8,128)S(1)}, f32[20,64,128]{2,1,0:T(8,128)S(1)}, u32[]{:S(2)}, u32[]{:S(2)}) collective-permute-start(f32[20,64,128]{2,1,0:T(8,128)S(1)} %slice_add_fusion.2), channel_id=1, source_target_pairs={{2,4},{4,2},{3,5},{5,3},{10,12},{12,10},{11,13},{13,11},{18,20},{2... | collective-permute-start | bytes 1966088 | tf_op jit(solution)/shard_map/cond/branch_0_fun/ppermute | solution.py:278
  148.6 14.9 %copy-start.45 = (f32[11,64,128]{2,1,0:T(8,128)S(1)}, f32[11,64,128]{2,1,0:T(8,128)}, u32[]{:S(2)}) copy-start(f32[11,64,128]{2,1,0:T(8,128)} %get-tuple-element.92) | copy-start | bytes 1081348 | tf_op jit(solution)/shard_map/cond
  148.6 33.7 %collective-permute-start.4 = (f32[11,64,128]{2,1,0:T(8,128)}, f32[11,64,128]{2,1,0:T(8,128)}, u32[]{:S(2)}, u32[]{:S(2)}) collective-permute-start(f32[11,64,128]{2,1,0:T(8,128)} %slice_add_fusion.7), channel_id=1, source_target_pairs={{4,6},{2,0},{5,7},{3,1},{12,14},{10,8},{13,15},{11,9},{20,22},{18,... | collective-permute-start | bytes 1081352 | tf_op jit(solution)/shard_map/cond/branch_0_fun/ppermute | solution.py:278
  160.6 19.2 %copy-start.29 = (f32[20,64,128]{2,1,0:T(8,128)S(1)}, f32[20,64,128]{2,1,0:T(8,128)}, u32[]{:S(2)}) copy-start(f32[20,64,128]{2,1,0:T(8,128)} %get-tuple-element.99) | copy-start | bytes 1966084 | tf_op jit(solution)/shard_map/cond
  162.7 27.4 %collective-permute-start.17 = (f32[20,64,128]{2,1,0:T(8,128)}, f32[20,64,128]{2,1,0:T(8,128)S(1)}, u32[]{:S(2)}, u32[]{:S(2)}) collective-permute-start(f32[20,64,128]{2,1,0:T(8,128)} %slice_add_fusion.1), channel_id=1, source_target_pairs={{2,4},{4,2},{3,5},{5,3},{10,12},{12,10},{11,13},{13,11},{18,20},{2... | collective-permute-start | bytes 1966088 | tf_op jit(solution)/shard_map/cond/branch_0_fun/ppermute | solution.py:278
  163.4 17.4 %copy-start.17 = (f32[20,64,128]{2,1,0:T(8,128)}, f32[20,64,128]{2,1,0:T(8,128)S(1)}, u32[]{:S(2)}) copy-start(f32[20,64,128]{2,1,0:T(8,128)S(1)} %collective-permute-done.10.refs_6_) | copy-start | bytes 1966084 | tf_op jit(solution)/shard_map/cond
  164.3 17.3 %copy-start.54 = (s32[3]{0:T(128)S(1)}, s32[3]{0:T(128)}, u32[]{:S(2)}) copy-start(s32[3]{0:T(128)} %constant.85) | copy-start | bytes 40 | tf_op jit(solution)/shard_map/cond
  164.3 17.9 %collective-permute-start.11 = (f32[11,64,128]{2,1,0:T(8,128)}, f32[11,64,128]{2,1,0:T(8,128)S(1)}, u32[]{:S(2)}, u32[]{:S(2)}) collective-permute-start(f32[11,64,128]{2,1,0:T(8,128)} %slice_add_fusion.6), channel_id=1, source_target_pairs={{4,6},{2,0},{5,7},{3,1},{12,14},{10,8},{13,15},{11,9},{20,22},{18,... | collective-permute-start | bytes 1081352 | tf_op jit(solution)/shard_map/cond/branch_0_fun/ppermute | solution.py:278
  179.8 6.8 %copy-start.9 = (f32[28,64,128]{2,1,0:T(8,128)}, f32[28,64,128]{2,1,0:T(8,128)S(1)}, u32[]{:S(2)}) copy-start(f32[28,64,128]{2,1,0:T(8,128)S(1)} %collective-permute-done.23.refs_5_) | copy-start | bytes 2752516 | tf_op jit(solution)/shard_map/cond
  180.9 11.9 %collective-permute-start.24 = (f32[20,64,128]{2,1,0:T(8,128)}, f32[20,64,128]{2,1,0:T(8,128)S(1)}, u32[]{:S(2)}, u32[]{:S(2)}) collective-permute-start(f32[20,64,128]{2,1,0:T(8,128)} %slice_add_fusion), channel_id=1, source_target_pairs={{2,4},{4,2},{3,5},{5,3},{10,12},{12,10},{11,13},{13,11},{18,20},{2... | collective-permute-start | bytes 1966088 | tf_op jit(solution)/shard_map/cond/branch_0_fun/ppermute | solution.py:278
  182.2 0.8 copy-start.46
  186.6 32.4 %all-to-all-start = ((f32[8,2,2,64,128]{4,3,2,1,0:T(8,128)}), f32[8,2,2,64,128]{4,3,2,1,0:T(8,128)S(1)}, u32[]{:S(2)}, u32[]{:S(2)}) async-start(f32[8,2,2,64,128]{4,3,2,1,0:T(8,128)} %branch_0_fun.9), calls=%async_computation | async-start | bytes 2097152 | tf_op jit(solution)/shard_map/cond/branch_0_fun/all_to_all | solution.py:283
  190.1 2.6 %copy-start.44 = (f32[11,64,128]{2,1,0:T(8,128)S(1)}, f32[11,64,128]{2,1,0:T(8,128)}, u32[]{:S(2)}) copy-start(f32[11,64,128]{2,1,0:T(8,128)} %get-tuple-element.100) | copy-start | bytes 1081348 | tf_op jit(solution)/shard_map/cond
  190.2 24.4 %copy-start.15 = (f32[20,64,128]{2,1,0:T(8,128)}, f32[20,64,128]{2,1,0:T(8,128)S(1)}, u32[]{:S(2)}) copy-start(f32[20,64,128]{2,1,0:T(8,128)S(1)} %collective-permute-done.17.refs_2_) | copy-start | bytes 1966084 | tf_op jit(solution)/shard_map/cond
  191.5 15.7 %collective-permute-start.18 = (f32[11,64,128]{2,1,0:T(8,128)S(1)}, f32[11,64,128]{2,1,0:T(8,128)S(1)}, u32[]{:S(2)}, u32[]{:S(2)}) collective-permute-start(f32[11,64,128]{2,1,0:T(8,128)S(1)} %slice_add_fusion.5), channel_id=1, source_target_pairs={{4,6},{2,0},{5,7},{3,1},{12,14},{10,8},{13,15},{11,9},{20,22},{18,... | collective-permute-start | bytes 1081352 | tf_op jit(solution)/shard_map/cond/branch_0_fun/ppermute | solution.py:278
  192.8 21.8 %copy-start.16 = (f32[20,64,128]{2,1,0:T(8,128)}, f32[20,64,128]{2,1,0:T(8,128)S(1)}, u32[]{:S(2)}) copy-start(f32[20,64,128]{2,1,0:T(8,128)S(1)} %collective-permute-done.24.refs_6_) | copy-start | bytes 1966084 | tf_op jit(solution)/shard_map/cond
  192.8 21.7 %collective-permute-start.25 = (f32[11,64,128]{2,1,0:T(8,128)S(1)}, f32[11,64,128]{2,1,0:T(8,128)S(1)}, u32[]{:S(2)}, u32[]{:S(2)}) collective-permute-start(f32[11,64,128]{2,1,0:T(8,128)S(1)} %slice_add_fusion.4), channel_id=1, source_target_pairs={{4,6},{2,0},{5,7},{3,1},{12,14},{10,8},{13,15},{11,9},{20,22},{18,... | collective-permute-start | bytes 1081352 | tf_op jit(solution)/shard_map/cond/branch_0_fun/ppermute | solution.py:278
  207.2 7.4 %copy-start.47 = (f32[11,64,128]{2,1,0:T(8,128)}, f32[11,64,128]{2,1,0:T(8,128)S(1)}, u32[]{:S(2)}) copy-start(f32[11,64,128]{2,1,0:T(8,128)S(1)} %collective-permute-done.18.refs_3_) | copy-start | bytes 1081348 | tf_op jit(solution)/shard_map/cond
  214.6 0.8 copy-start.48
  218.9 19.6 %copy-start.3 = (f32[8,2,2,64,128]{4,3,2,1,0:T(8,128)}, f32[8,2,2,64,128]{4,3,2,1,0:T(8,128)S(1)}, u32[]{:S(2)}) copy-start(f32[8,2,2,64,128]{4,3,2,1,0:T(8,128)S(1)} %all-to-all-done.refs_0_) | copy-start | bytes 3145732 | tf_op jit(solution)/shard_map/cond

commit v3 on v2

--- a/solution.py
+++ b/solution.py
@@ -17,34 +17,83 @@
     return hi, lo
 
 
-def product_kernel(dims, outs, meta_ref, pairs_ref, index_ref, s_ref, *refs):
-    blocks, h, kc, ys, rb, cb, n_pairs = dims
-    pieces, lists, (s_cat, j_cat, part) = refs[:4], refs[4 : 4 + outs], refs[4 + outs :]
-    core = meta_ref[0]
-    q = h // 2
-
-    def put(target, row, y, x, right):
-        hi, lo = split_hi_lo(x)
-        base = 3 * kc * y
-        rows = pl.ds(pl.multiple_of(row, q), x.shape[0])
-        target[rows, base : base + kc] = hi
-        target[rows, base + kc : base + 2 * kc] = lo if right else hi
-        target[rows, base + 2 * kc : base + 3 * kc] = hi if right else lo
+def put_parts(target, row, y, x, order):
+    parts = split_hi_lo(x)
+    kc = x.shape[1]
+    rows = pl.ds(pl.multiple_of(row, x.shape[0]), x.shape[0])
+    for at, which in enumerate(order):
+        col = (3 * y + at) * kc
+        target[rows, col : col + kc] = parts[which]
+
+
+def put_right(core, pieces, right):
+    ys, blocks, q, _ = pieces[0].shape
 
     @pl.loop(0, blocks)
     def _(j):
         for y in range(ys):
-            put(s_cat, j * h, y, s_ref[y, j], False)
             for at, piece in enumerate(pieces):
                 side = core if at % 2 == 0 else 1 - core
-                put(j_cat, j * 2 * h + (at // 2 * 2 + side) * q, y, piece[y, j], True)
+                put_parts(right, (4 * j + at // 2 * 2 + side) * q, y, piece[y, j], (0, 1, 0))
+
+
+def prepare_kernel(meta_ref, *refs):
+    put_right(meta_ref[0], refs[:4], refs[4])
+
+
+def prepare(meta, pieces):
+    ys, blocks, q, kc = pieces[0].shape
+    vmem = pl.BlockSpec(memory_space=pltpu.VMEM)
+    return pl.pallas_call(
+        prepare_kernel,
+        out_shape=jax.ShapeDtypeStruct((blocks * 4 * q, 3 * kc * ys), jnp.bfloat16),
+        in_specs=[pl.BlockSpec(memory_space=pltpu.SMEM)] + [vmem] * 4,
+        out_specs=vmem,
+        cost_estimate=pl.CostEstimate(flops=2**28, bytes_accessed=40 * pieces[0].size, transcendentals=0),
+    )(meta, *pieces)
+
+
+def product_kernel(dims, outs, first, meta_ref, pairs_ref, index_ref, *refs):
+    blocks, h, _, ys, rb, cb, n_pairs = dims
+    n_in = 4 if first else 3
+    hbm, lists, (left, part, right, sems, *held) = refs[:n_in], refs[n_in:][:outs], refs[n_in + outs :]
+    q = h // 2
+
+    def right_copy(jb):
+        rows = pl.ds(pl.multiple_of(jb * cb, cb), cb)
+        return pltpu.make_async_copy(hbm[2].at[rows], right.at[rows], sems.at[2 + jb])
+
+    copies = [pltpu.make_async_copy(hbm[i], held[i], sems.at[i]) for i in range(len(held))]
+    for copy in copies:
+        copy.start()
+    if not first:
+        for jb in range(right.shape[0] // cb):
+            right_copy(jb).start()
+    for copy in copies[:2]:
+        copy.wait()
+
+    @pl.loop(0, blocks)
+    def _(i):
+        for y in range(ys):
+            for slot in range(2):
+                put_parts(left, i * h + slot * q, y, held[slot][y, i], (0, 0, 1))
+
+    if first:
+        for copy in copies[2:]:
+            copy.wait()
+        put_right(meta_ref[0], (held[0], held[2], held[1], held[3]), right)
 
     @pl.loop(0, n_pairs)
     def _(t):
-        ib, jb = pairs_ref[2 * t], pairs_ref[2 * t + 1]
-        left = s_cat[pl.ds(pl.multiple_of(ib * rb, rb), rb), :]
-        right = j_cat[pl.ds(pl.multiple_of(jb * cb, cb), cb), :]
-        out = lax.dot_general(left, right, (((1,), (1,)), ((), ())), preferred_element_type=jnp.float32)
+        ib, jb = pairs_ref[3 * t], pairs_ref[3 * t + 1]
+        if not first:
+
+            @pl.when(pairs_ref[3 * t + 2] == 1)
+            def _():
+                right_copy(jb).wait()
+
+        rows, cols = pl.ds(pl.multiple_of(ib * rb, rb), rb), pl.ds(pl.multiple_of(jb * cb, cb), cb)
+        out = lax.dot_general(left[rows, :], right[cols, :], (((1,), (1,)), ((), ())), preferred_element_type=jnp.float32)
         for a in range(rb // h):
             for b in range(cb // (2 * h)):
                 where = (ib * (rb // h) + a) * blocks + jb * (cb // (2 * h)) + b
@@ -60,24 +109,26 @@
         base += one.shape[0]
 
 
-def products(dims, sizes, meta, pairs, index, s, pieces):
+def products(dims, sizes, meta, pairs, index, pieces, rights):
     blocks, h, kc, ys, rb, cb, n_pairs = dims
-    outs = len(sizes)
     k3 = 3 * kc * ys
+    first = len(rights) == 2
     smem, vmem = pl.BlockSpec(memory_space=pltpu.SMEM), pl.BlockSpec(memory_space=pltpu.VMEM)
     flops = 2 * n_pairs * rb * cb * k3
     return pl.pallas_call(
-        functools.partial(product_kernel, dims, outs),
+        functools.partial(product_kernel, dims, len(sizes), first),
         out_shape=[jax.ShapeDtypeStruct((size, h, 2 * h), jnp.float32) for size in sizes],
-        in_specs=[smem] * 3 + [vmem] * 5,
-        out_specs=[vmem] * outs,
+        in_specs=[smem] * 3 + [pl.BlockSpec(memory_space=pl.ANY)] * (2 + len(rights)),
+        out_specs=[vmem] * len(sizes),
         scratch_shapes=[
             pltpu.VMEM((blocks * h, k3), jnp.bfloat16),
+            pltpu.VMEM((blocks * blocks, h, 2 * h), jnp.float32),
             pltpu.VMEM((blocks * 2 * h, k3), jnp.bfloat16),
-            pltpu.VMEM((blocks * blocks, h, 2 * h), jnp.float32),
+            pltpu.SemaphoreType.DMA((max(4, 2 + blocks * 2 * h // cb),)),
+            *[pltpu.VMEM(pieces[0].shape, jnp.float32)] * (4 if first else 2),
         ],
-        cost_estimate=pl.CostEstimate(flops=flops, bytes_accessed=8 * s.size * 4, transcendentals=0),
-    )(meta, pairs, index, s, *pieces)
+        cost_estimate=pl.CostEstimate(flops=flops, bytes_accessed=4 * blocks * h * k3, transcendentals=0),
+    )(meta, pairs, index, *pieces, *rights)
 
 
 def pick_kernel(chunks, spread_ref, live_ref, *refs):
@@ -113,20 +164,9 @@
     in_refs, out_ref = refs[:-1], refs[-1]
     h, w = in_refs[0].shape[3:]
     q = h // 2
-    for source, chip, side, parts in plan:
-        for col, spots in parts:
-            cols = slice(col * w, (col + 1) * w)
-            first, second = spots[0][0], spots[1][0]
-            for half in range(2):
-                row = chip * w + half * h + side * q
-                rows = slice(half * q, (half + 1) * q)
-                if first == second:
-                    out_ref[:, row : row + q, cols] = in_refs[first[0]][source, first[1], :, rows, :]
-                else:
-                    halves = []
-                    for (group, at), spot in spots:
-                        halves.append(in_refs[group][source, at, :, rows, spot * h : (spot + 1) * h])
-                    out_ref[:, row : row + q, cols] = jnp.concatenate(halves, axis=2)
+    for source, group, at, slot, row, col in plan:
+        rows = slice(slot * q, (slot + 1) * q)
+        out_ref[:, row : row + q, col : col + w] = in_refs[group][source, at, :, rows, :]
 
 
 def place(plan, arrived):
@@ -175,8 +215,11 @@
     for c in range(len(chunks)):
         events.append((gap * c, "product", c, 0))
         events.extend((gap * c + 2 * step - 1.8 + 0.01 * step, "step", c, step) for step in range(2, zs))
-        if c:
-            events.append((gap * c - 0.5, "fetch", c, 0))
+    if len(chunks) > 1:
+        events.append((0.1, "prepare", 0, 0))
+    for u in range(1, chips):
+        if u not in singles:
+            events.extend((gap * (1 + half) + 0.1 - 0.2 * half, "chip", u, half) for half in range(2))
     groups = [list(range(c, min(c + 2, len(chunks)))) for c in range(0, len(chunks), 2)]
     events.extend((gap * group[-1] + 2 * zs - 1.7, "early", at, 0) for at, group in enumerate(groups[:-1]))
     events.sort(key=lambda e: e[0])
@@ -200,12 +243,10 @@
     h = BLOCK // plane
     rb, cb = min(WIDE, blocks * h), min(2 * WIDE, blocks * 2 * h)
     per_i, per_j = rb // h, cb // (2 * h)
-    pair_list = [
-        (ib, jb)
-        for ib in range(blocks // per_i)
-        for jb in range(blocks // per_j)
-        if ib * per_i + per_i - 1 >= jb * per_j
-    ]
+    pair_list = []
+    for jb in range(blocks // per_j):
+        rows = [ib for ib in range(blocks // per_i) if ib * per_i + per_i - 1 >= jb * per_j]
+        pair_list += [(ib, jb, int(ib == rows[0])) for ib in rows]
     dims = (blocks, h, kc, ys, rb, cb, len(pair_list))
     pairs = jnp.array([v for pair in pair_list for v in pair], jnp.int32)
     my_z, my_row, my_y = (lax.axis_index(name) for name in ("z", "row", "y"))
@@ -256,9 +297,6 @@
     def run_scoped(sizes, s, index, spread, my_tile, my_live):
         same, peer = {(0, 0): s[:, :, : h // 2], (0, 1): s[:, :, h // 2 :]}, {}
 
-        def cores(u, half):
-            peer[u, half] = core_swap(same[u, half])
-
         def reach(u, half):
             if (u, half) not in same:
                 low = link_of(u, half)
@@ -266,13 +304,13 @@
                 same[u, half] = chip_swap(same[u ^ low, half], low)
 
         for half in range(2):
-            cores(0, half)
+            peer[half] = core_swap(same[0, half])
             for u in range(1, chips):
                 reach(u, half)
         flat_index = jnp.concatenate([index[i, :size] for i, size in enumerate(sizes)] + [my_tile])
         limit = jnp.array(sizes, jnp.int32)[:, None] - 1
         flat_spread = jnp.minimum(spread, limit).reshape(-1)
-        lists, flows, arrived = {}, {}, []
+        lists, flows, arrived, rights = {}, {}, [], (peer[0], peer[1])
 
         def forward(c, step, x):
             flows[c, step] = lax.ppermute(x, "z", [(step - 1, step), (zs - step, zs - step - 1)])
@@ -283,33 +321,28 @@
             arrived.append(lax.all_to_all(ready, ("y", "row"), 0, 0, tiled=True))
 
         for _, kind, c, step in events:
-            if kind == "fetch":
-                for u, half in chunks[c]:
-                    cores(u, half)
+            if kind == "prepare":
+                rights = (prepare(meta, (same[0, 0], peer[0], same[0, 1], peer[1])),)
             elif kind == "product":
-                pieces = [side[key] for key in chunks[c] for side in (same, peer)]
-                lists[c] = products(dims, (*sizes, entries), meta, pairs, flat_index, s, pieces)
+                pieces = [same[key] for key in chunks[c]]
+                lists[c] = products(dims, (*sizes, entries), meta, pairs, flat_index, pieces, rights)
                 forward(c, 1, lists[c][0])
             elif kind == "step":
                 own = lists[c][step - 1]
                 passed = flows[c, step - 1][: own.shape[0]] + own
                 forward(c, step, passed)
-            else:
+            elif kind == "early":
                 deliver(groups[c])
 
         deliver(groups[-1])
         plan = []
         for d in range(plane):
-            chip = (d % rows_n) // 2 * ys + d // rows_n
-            parts = []
-            for u in range(chips):
-                spots = []
-                for half in range(2):
-                    c = next(i for i, chunk in enumerate(chunks) if (u, half) in chunk)
-                    where = next((g, group.index(c)) for g, group in enumerate(groups) if c in group)
-                    spots.append((where, chunks[c].index((u, half))))
-                parts.append((chip ^ u, tuple(spots)))
-            plan.append((d, chip, d % 2, tuple(parts)))
+            chip = d % rows_n // 2 * ys + d // rows_n
+            for g, group in enumerate(groups):
+                for at, c in enumerate(group):
+                    for slot, (u, half) in enumerate(chunks[c]):
+                        row = (chip ^ u) * 2 * h + half * h + d % 2 * (h // 2)
+                        plan.append((d, g, at, slot, row, chip * 2 * h))
         return place(tuple(plan), arrived)[None]
 
     mean = [-(-tiles * (zs - step) // zs) for step in range(1, zs)]

time: 243 us -> 223 us (0.918)
  waiting for transfers between devices: 119 us -> 91.8 us
  Pallas kernels: 42.4 us -> 47.6 us
  local copies, waits for them, and re-layouts: 7.21 us -> 10.6 us
    ppermute x3, waiting for transfers between devices: 24.3 us -> 8.61 us  [chip_swap(): return lax.ppermute(x, 'row', [(r, r ^ 2 * ux) for r in range(rows_n)])]
    ppermute x3, waiting for transfers between devices: 29.7 us -> 22.4 us  [chip_swap(): return lax.ppermute(x, 'y', [(y, y ^ uy) for y in range(ys)])]
    pallas_call x4 -> x5, Pallas kernels: 32 us -> 38.7 us  [the longest x4 33.4 us: products(): pl.pallas_call(functools.partial(product_kernel, dims, len(sizes), first)...]
    ppermute x12, waiting for transfers between devices: 45.2 us -> 40.7 us  [forward(): lax.ppermute(x, 'z', [(step - 1, step), (zs - step, zs - step - 1)])]
  transfers between devices with their start and end apart: 28 -> 22, of which waited for: 10 -> 8; matrix products, arithmetic and copies ran while one was open for 6% -> 6% of each run, Pallas kernels for 16% -> 21%
where the time goes in v3:
time: 223 us; the launch traced here: 222 us
  waiting for transfers between devices  91.8 us (41%)
  Pallas kernels  47.6 us (21%)
  starting transfers between devices  37.5 us (17%)
  blocking collectives  19.6 us (9%)
  other arithmetic  11.1 us (5%)
  local copies, waits for them, and re-layouts  10.6 us (5%)
  between operations  3.76 us (2%)
    ppermute x12, waiting for transfers between devices, forward(): lax.ppermute(x, 'z', [(step - 1, step), (zs - step, zs - step - 1)])  40.7 us
    pallas_call x4, Pallas kernels, products(): pl.pallas_call(functools.partial(product_kernel, dims, len(sizes), first)...  33.4 us
    ppermute x3, waiting for transfers between devices, chip_swap(): return lax.ppermute(x, 'y', [(y, y ^ uy) for y in range(ys)])  22.4 us
    ppermute x12, starting transfers between devices, forward(): lax.ppermute(x, 'z', [(step - 1, step), (zs - step, zs - step - 1)])  21.8 us
    all_to_all x1, waiting for transfers between devices, body(): lax.all_to_all(sliced, ('y', 'row'), 0, 0, tiled=True)  20 us
    all_to_all x1, blocking collectives, deliver(): arrived.append(lax.all_to_all(ready, ('y', 'row'), 0, 0, tiled=True))  19.6 us
    add x8, other arithmetic, run_scoped(): passed = flows[c, step - 1][:own.shape[0]] + own  9.2 us
    ppermute x3, waiting for transfers between devices, chip_swap(): return lax.ppermute(x, 'row', [(r, r ^ 2 * ux) for r in range(rows_n)])  8.61 us
  transfers between devices with their start and end apart: 22, of which 8 were waited for; matrix products, arithmetic and copies ran while one was open for 6% of the time, Pallas kernels for 21%

profile of v3, /device:TPU:0, one launch (start us, length us, event | category | flops | bytes accessed | tf_op | source)
XLA Modules:
  0.0 222.5 jit_solution(4372804776943966951)
XLA Ops:
  0.0 3.2 %copy.47 = f32[2,2,2,2,2,32,512]{6,5,4,3,2,1,0:T(8,128)} copy(f32[2,2,2,2,2,32,512]{6,5,2,4,0,1,3:T(8,128)} %bitcast.52) | data formatting | bytes 4194304 | tf_op jit(solution)/shard_map/transpose | solution.py:254
  3.2 5.3 %all-to-all-start.6 = ((f32[8,2,64,512]{3,2,1,0:T(8,128)}), f32[8,2,64,512]{3,2,1,0:T(8,128)S(1)}, u32[]{:S(2)}, u32[]{:S(2)}) async-start(f32[8,2,64,512]{3,2,1,0:T(8,128)} %bitcast.51), calls=%async_computation.6 | async-start | bytes 4194304 | tf_op jit(solution)/shard_map/all_to_all | solution.py:256
  8.7 0.1 select_reduce_fusion.2
  8.9 0.2 reduce_sum.121
  9.1 0.2 select_reduce_fusion.8
  9.2 0.7 fusion.12
  13.7 0.1 copy.40
  13.9 0.1 copy.44
  14.2 0.1 copy.46
  14.4 0.1 copy.48
  14.7 0.2 select_reduce_fusion.3
  15.0 0.1 select_reduce_fusion
  15.1 20.0 %all-to-all-done.6 = f32[8,2,64,512]{3,2,1,0:T(8,128)S(1)} async-done(((f32[8,2,64,512]{3,2,1,0:T(8,128)}), f32[8,2,64,512]{3,2,1,0:T(8,128)S(1)}, u32[]{:S(2)}, u32[]{:S(2)}) %all-to-all-start.6) | async-done | bytes 2097184 | tf_op jit(solution)/shard_map/all_to_all | solution.py:256
  35.1 186.0 %conditional.1 = (f32[1,2,512,512]{3,2,1,0:T(8,128)S(1)}) conditional(s32[]{:T(128)} %bitcast.12, ((), s32[3,16]{1,0:T(4,128)S(1)}, s32[1,36]{1,0:T(1,128)S(1)}, s32[1,36]{1,0:T(1,128)S(1)}, s32[1,36]{1,0:T(1,128)S(1)}, /*index=5*/s32[16]{0:T(128)S(1)}, f32[2,8,64,512]{3,2,1,0:T(8,128)S(1)}, s32[2]{0:T(128)S(1)}, ...), branch_computations={%region_13.14_spmd, %region_14.15_spmd, %region_15.16_spmd} | conditional | flops 9933684736 | bytes 200285856 | solution.py:357
  35.1 1.2 fusion.9
  36.4 0.5 collective-permute-start.1
  36.9 0.5 collective-permute-start.5
  37.4 0.7 collective-permute-start.6
  38.0 1.4 collective-permute-start.11
  39.4 1.6 collective-permute-start.10
  41.0 0.6 pad_add_fusion.index_ref
  41.6 1.0 copy-done.27
  42.6 8.4 %branch_0_fun.8 = (f32[28,64,128]{2,1,0:T(8,128)}, f32[20,64,128]{2,1,0:T(8,128)}, f32[11,64,128]{2,1,0:T(8,128)}, f32[16,64,128]{2,1,0:T(8,128)}) custom-call(s32[2]{0:T(128)S(1)} %get-tuple-element.78.meta_ref, s32[9]{0:T(128)S(1)} %get-tuple-element.79.pairs_ref, s32[75]{0:T(128)} %pad_add_fusion.index_ref, f32[2,8,32,512]{3,2,1,0:T(8,128)} %get-tuple-element.176.refs_0_, ...), custom_call_target="tpu_custom_call" | custom-call | flops 2415919104 | bytes 6291456 | tf_op jit(solution)/shard_map/cond/branch_0_fun/pallas_call | solution.py:118
  51.1 3.5 %collective-permute-start.2 = (f32[28,64,128]{2,1,0:T(8,128)}, f32[28,64,128]{2,1,0:T(8,128)S(1)}, u32[]{:S(2)}, u32[]{:S(2)}) collective-permute-start(f32[28,64,128]{2,1,0:T(8,128)} %get-tuple-element.86), channel_id=1, source_target_pairs={{0,2},{6,4},{1,3},{7,5},{8,10},{14,12},{9,11},{15,13},{16,18},{22,... | collective-permute-start | bytes 2752520 | tf_op jit(solution)/shard_map/cond/branch_0_fun/ppermute | solution.py:316
  54.6 8.6 %collective-permute-done.5.refs_0_ = f32[2,8,32,512]{3,2,1,0:T(8,128)} collective-permute-done((f32[2,8,32,512]{3,2,1,0:T(8,128)}, f32[2,8,32,512]{3,2,1,0:T(8,128)}, u32[]{:S(2)}, u32[]{:S(2)}) %collective-permute-start.5) | collective-permute-done | bytes 1048608 | tf_op jit(solution)/shard_map/cond/branch_0_fun/ppermute | solution.py:283
  63.2 0.6 collective-permute-start.15
  63.8 22.4 %collective-permute-done.11.refs_1_ = f32[2,8,32,512]{3,2,1,0:T(8,128)} collective-permute-done((f32[2,8,32,512]{3,2,1,0:T(8,128)S(1)}, f32[2,8,32,512]{3,2,1,0:T(8,128)}, u32[]{:S(2)}, u32[]{:S(2)}) %collective-permute-start.11) | collective-permute-done | bytes 1048608 | tf_op jit(solution)/shard_map/cond/branch_0_fun/ppermute | solution.py:285
  86.2 1.5 collective-permute-start.16
  87.7 5.3 %branch_0_fun.9.refs_2_ = bf16[1024,3072]{1,0:T(8,128)(2,1)} custom-call(s32[2]{0:T(128)S(1)} %get-tuple-element.78.meta_ref, f32[2,8,32,512]{3,2,1,0:T(8,128)} %get-tuple-element.176.refs_0_, f32[2,8,32,512]{3,2,1,0:T(8,128)} %copy-done.25, f32[2,8,32,512]{3,2,1,0:T(8,128)} %copy-done.7, f32[2,8,32,512]{3,2,1,0:T(8,128)} %copy-done.27), custom_call_target="tpu_custom_call" | custom-call | flops 268435456 | bytes 10485760 | tf_op jit(solution)/shard_map/cond/branch_0_fun/pallas_call | solution.py:47
  93.0 8.3 %branch_0_fun.10 = (f32[28,64,128]{2,1,0:T(8,128)}, f32[20,64,128]{2,1,0:T(8,128)}, f32[11,64,128]{2,1,0:T(8,128)}, f32[16,64,128]{2,1,0:T(8,128)}) custom-call(s32[2]{0:T(128)S(1)} %get-tuple-element.78.meta_ref, s32[9]{0:T(128)S(1)} %get-tuple-element.79.pairs_ref, s32[75]{0:T(128)} %pad_add_fusion.index_ref, ...), custom_call_target="tpu_custom_call" | custom-call | flops 2415919104 | bytes 6291456 | tf_op jit(solution)/shard_map/cond/branch_0_fun/pallas_call | solution.py:118
  101.3 4.4 %collective-permute-start.7 = (f32[28,64,128]{2,1,0:T(8,128)}, f32[28,64,128]{2,1,0:T(8,128)}, u32[]{:S(2)}, u32[]{:S(2)}) collective-permute-start(f32[28,64,128]{2,1,0:T(8,128)} %get-tuple-element.90), channel_id=1, source_target_pairs={{0,2},{6,4},{1,3},{7,5},{8,10},{14,12},{9,11},{15,13},{16,18},{22,... | collective-permute-start | bytes 2752520 | tf_op jit(solution)/shard_map/cond/branch_0_fun/ppermute | solution.py:316
  105.7 8.3 %branch_0_fun.12 = (f32[28,64,128]{2,1,0:T(8,128)}, f32[20,64,128]{2,1,0:T(8,128)}, f32[11,64,128]{2,1,0:T(8,128)}, f32[16,64,128]{2,1,0:T(8,128)}) custom-call(s32[2]{0:T(128)S(1)} %get-tuple-element.78.meta_ref, s32[9]{0:T(128)S(1)} %get-tuple-element.79.pairs_ref, s32[75]{0:T(128)} %pad_add_fusion.index_ref, ...), custom_call_target="tpu_custom_call" | custom-call | flops 2415919104 | bytes 6291456 | tf_op jit(solution)/shard_map/cond/branch_0_fun/pallas_call | solution.py:118
  114.0 1.3 collective-permute-start.12
  115.4 2.3 %slice_add_fusion.3 = f32[20,64,128]{2,1,0:T(8,128)} fusion(f32[20,64,128]{2,1,0:T(8,128)} %get-tuple-element.87, f32[28,64,128]{2,1,0:T(8,128)S(1)} %collective-permute-done.2.refs_1_), kind=kLoop, calls=%fused_computation.3 | loop fusion | flops 163840 | bytes 1966080 | tf_op jit(solution)/shard_map/cond/branch_0_fun/add | solution.py:332
  117.8 1.6 collective-permute-start.3
  119.4 8.3 %branch_0_fun.13 = (f32[28,64,128]{2,1,0:T(8,128)}, f32[20,64,128]{2,1,0:T(8,128)}, f32[11,64,128]{2,1,0:T(8,128)}, f32[16,64,128]{2,1,0:T(8,128)}) custom-call(s32[2]{0:T(128)} %copy-done.57, s32[9]{0:T(128)} %copy-done.70, s32[75]{0:T(128)} %pad_add_fusion.index_ref, f32[2,8,32,512]{3,2,1,0:T(8,128)} %collective-permute-done.15.refs_0_, ...), custom_call_target="tpu_custom_call" | custom-call | flops 2415919104 | bytes 6291456 | tf_op jit(solution)/shard_map/cond/branch_0_fun/pallas_call | solution.py:118
  127.8 2.5 %collective-permute-start.17 = (f32[28,64,128]{2,1,0:T(8,128)}, f32[28,64,128]{2,1,0:T(8,128)S(1)}, u32[]{:S(2)}, u32[]{:S(2)}) collective-permute-start(f32[28,64,128]{2,1,0:T(8,128)} %get-tuple-element.98), channel_id=1, source_target_pairs={{0,2},{6,4},{1,3},{7,5},{8,10},{14,12},{9,11},{15,13},{16,18},{22,... | collective-permute-start | bytes 2752520 | tf_op jit(solution)/shard_map/cond/branch_0_fun/ppermute | solution.py:316
  130.3 1.2 slice_add_fusion.2
  131.6 0.8 collective-permute-start.8
  132.4 13.1 %collective-permute-done.12.refs_1_ = f32[28,64,128]{2,1,0:T(8,128)S(1)} collective-permute-done((f32[28,64,128]{2,1,0:T(8,128)}, f32[28,64,128]{2,1,0:T(8,128)S(1)}, u32[]{:S(2)}, u32[]{:S(2)}) %collective-permute-start.12) | collective-permute-done | bytes 917536 | tf_op jit(solution)/shard_map/cond/branch_0_fun/ppermute | solution.py:316
  145.5 1.0 slice_add_fusion.1
  146.5 0.8 collective-permute-start.13
  147.3 1.8 slice_add_fusion.7
  149.1 1.3 collective-permute-start.4
  150.4 0.9 slice_add_fusion.6
  151.2 1.3 collective-permute-start.9
  152.5 9.0 %collective-permute-done.17.refs_5_ = f32[28,64,128]{2,1,0:T(8,128)S(1)} collective-permute-done((f32[28,64,128]{2,1,0:T(8,128)}, f32[28,64,128]{2,1,0:T(8,128)S(1)}, u32[]{:S(2)}, u32[]{:S(2)}) %collective-permute-start.17) | collective-permute-done | bytes 917536 | tf_op jit(solution)/shard_map/cond/branch_0_fun/ppermute | solution.py:316
  161.5 1.0 slice_add_fusion
  162.5 1.5 collective-permute-start.18
  164.1 0.7 reshape.246.spread_ref
  164.8 0.2 collective-permute-done.9.refs_7_
  165.0 0.7 copy-done.52
  165.7 3.6 %branch_0_fun.11 = f32[8,2,2,64,128]{4,3,2,1,0:T(8,128)} custom-call(s32[48]{0:T(128)} %reshape.246.spread_ref, s32[16]{0:T(128)S(1)} %get-tuple-element.77.live_ref, f32[16,64,128]{2,1,0:T(8,128)} %get-tuple-element.85.refs_0_, f32[28,64,128]{2,1,0:T(8,128)} %copy-done.13, f32[20,64,128]{2,1,0:T(8,128)} %collective-permute-done.3.refs_2_, ...), custom_call_target="tpu_custom_call" | custom-call | tf_op jit(solution)/shard_map/cond/branch_0_fun/pallas_call | solution.py:155
  169.3 3.7 %all-to-all-start = ((f32[8,2,2,64,128]{4,3,2,1,0:T(8,128)}), f32[8,2,2,64,128]{4,3,2,1,0:T(8,128)S(1)}, u32[]{:S(2)}, u32[]{:S(2)}) async-start(f32[8,2,2,64,128]{4,3,2,1,0:T(8,128)} %branch_0_fun.11), calls=%async_computation | async-start | bytes 2097152 | tf_op jit(solution)/shard_map/cond/branch_0_fun/all_to_all | solution.py:321
  173.1 1.3 collective-permute-start.14
  174.4 1.0 slice_add_fusion.4
  175.5 1.3 collective-permute-start.19
  176.8 11.0 %collective-permute-done.14.refs_3_ = f32[11,64,128]{2,1,0:T(8,128)S(1)} collective-permute-done((f32[11,64,128]{2,1,0:T(8,128)S(1)}, f32[11,64,128]{2,1,0:T(8,128)S(1)}, u32[]{:S(2)}, u32[]{:S(2)}) %collective-permute-start.14) | collective-permute-done | bytes 360480 | tf_op jit(solution)/shard_map/cond/branch_0_fun/ppermute | solution.py:316
  187.8 7.4 %collective-permute-done.19.refs_7_ = f32[11,64,128]{2,1,0:T(8,128)S(1)} collective-permute-done((f32[11,64,128]{2,1,0:T(8,128)S(1)}, f32[11,64,128]{2,1,0:T(8,128)S(1)}, u32[]{:S(2)}, u32[]{:S(2)}) %collective-permute-start.19) | collective-permute-done | bytes 360480 | tf_op jit(solution)/shard_map/cond/branch_0_fun/ppermute | solution.py:316
  195.2 0.7 copy-done.54
  195.9 3.6 %branch_0_fun.14 = f32[8,2,2,64,128]{4,3,2,1,0:T(8,128)} custom-call(s32[48]{0:T(128)} %reshape.246.spread_ref, s32[16]{0:T(128)S(1)} %get-tuple-element.77.live_ref, f32[16,64,128]{2,1,0:T(8,128)} %get-tuple-element.93.refs_0_, f32[28,64,128]{2,1,0:T(8,128)} %copy-done.14, f32[20,64,128]{2,1,0:T(8,128)} %copy-done.21, f32[11,64,128]{2,1,0:T(8,128)} %copy-done.53, ...), custom_call_target="tpu_custom_call" | custom-call | tf_op jit(solution)/shard_map/cond/branch_0_fun/pallas_call | solution.py:155
  199.5 19.6 %all_to_all.29.refs_1_ = f32[8,2,2,64,128]{4,3,2,1,0:T(8,128)} all-to-all(f32[8,2,2,64,128]{4,3,2,1,0:T(8,128)} %branch_0_fun.14), channel_id=1, replica_groups=mesh['row'=4,'z'=4,'y'=2] {'y','row'}, dimensions={0} | all-to-all | bytes 2097152 | tf_op jit(solution)/shard_map/cond/branch_0_fun/all_to_all | solution.py:321
  219.1 1.8 branch_0_fun.15
  221.2 1.3 copy-done.18
  (86 shorter events, 1.3 us)
Async XLA Ops:
  3.2 5.5 %copy-start.61 = (s32[8,8]{1,0:T(8,128)S(1)}, s32[8,8]{1,0:T(8,128)}, u32[]{:S(2)}) copy-start(s32[8,8]{1,0:T(8,128)} %param.10) | copy-start | bytes 772
  3.2 31.9 %copy-start.69 = (s32[9]{0:T(128)S(1)}, s32[9]{0:T(128)}, u32[]{:S(2)}) copy-start(s32[9]{0:T(128)} %constant.79.clone) | copy-start | bytes 112
  3.2 31.9 %all-to-all-start.6 = ((f32[8,2,64,512]{3,2,1,0:T(8,128)}), f32[8,2,64,512]{3,2,1,0:T(8,128)S(1)}, u32[]{:S(2)}, u32[]{:S(2)}) async-start(f32[8,2,64,512]{3,2,1,0:T(8,128)} %bitcast.51), calls=%async_computation.6 | async-start | bytes 4194304 | tf_op jit(solution)/shard_map/all_to_all | solution.py:256
  35.1 70.6 %copy-start.57 = (s32[2]{0:T(128)}, s32[2]{0:T(128)S(1)}, u32[]{:S(2)}) copy-start(s32[2]{0:T(128)S(1)} %get-tuple-element.78.meta_ref) | copy-start | bytes 28 | tf_op jit(solution)/shard_map/cond
  35.1 70.6 %copy-start.70 = (s32[9]{0:T(128)}, s32[9]{0:T(128)S(1)}, u32[]{:S(2)}) copy-start(s32[9]{0:T(128)S(1)} %get-tuple-element.79.pairs_ref) | copy-start | bytes 112 | tf_op jit(solution)/shard_map/cond
  36.4 6.3 %copy-start.7 = (f32[2,8,32,512]{3,2,1,0:T(8,128)}, f32[2,8,32,512]{3,2,1,0:T(8,128)S(1)}, u32[]{:S(2)}) copy-start(f32[2,8,32,512]{3,2,1,0:T(8,128)S(1)} %get-tuple-element.175.refs_1_.refs_2_) | copy-start | bytes 3145732 | tf_op jit(solution)/shard_map/cond
  36.4 3.1 %collective-permute-start = (f32[2,8,32,512]{3,2,1,0:T(8,128)}, f32[2,8,32,512]{3,2,1,0:T(8,128)S(1)}, u32[]{:S(2)}, u32[]{:S(2)}) collective-permute-start(f32[2,8,32,512]{3,2,1,0:T(8,128)} %get-tuple-element.176.refs_0_), channel_id=1, source_target_pairs={{0,8},{8,0},{16,24},{24,16},{1,9},{9,1},{17,25},{25,17},{2,10},{10... | collective-permute-start | bytes 3145736 | tf_op jit(solution)/shard_map/cond/branch_0_fun/ppermute | solution.py:290
  36.4 5.3 %collective-permute-start.1 = (f32[2,8,32,512]{3,2,1,0:T(8,128)S(1)}, f32[2,8,32,512]{3,2,1,0:T(8,128)S(1)}, u32[]{:S(2)}, u32[]{:S(2)}) collective-permute-start(f32[2,8,32,512]{3,2,1,0:T(8,128)S(1)} %get-tuple-element.175.refs_1_.refs_2_), channel_id=1, source_target_pairs={{0,8},{8,0},{16,24},{24,16},{1,9},{9,1},{17,25},{25,17},{2,10},{10... | collective-permute-start | bytes 3145736 | tf_op jit(solution)/shard_map/cond/branch_0_fun/ppermute | solution.py:290
  36.9 26.3 %collective-permute-start.5 = (f32[2,8,32,512]{3,2,1,0:T(8,128)}, f32[2,8,32,512]{3,2,1,0:T(8,128)}, u32[]{:S(2)}, u32[]{:S(2)}) collective-permute-start(f32[2,8,32,512]{3,2,1,0:T(8,128)} %get-tuple-element.176.refs_0_), channel_id=1, source_target_pairs={{0,16},{8,24},{16,0},{24,8},{1,17},{9,25},{17,1},{25,9},{2,18},{10... | collective-permute-start | bytes 3145736 | tf_op jit(solution)/shard_map/cond/branch_0_fun/ppermute | solution.py:283
  37.4 55.6 %collective-permute-start.6 = (f32[2,8,32,512]{3,2,1,0:T(8,128)}, f32[2,8,32,512]{3,2,1,0:T(8,128)}, u32[]{:S(2)}, u32[]{:S(2)}) collective-permute-start(f32[2,8,32,512]{3,2,1,0:T(8,128)} %get-tuple-element.176.refs_0_), channel_id=1, source_target_pairs={{0,1},{1,0},{2,3},{3,2},{4,5},{5,4},{6,7},{7,6},{8,9},{9,8},{10,11... | collective-permute-start | bytes 3145736 | tf_op jit(solution)/shard_map/cond/branch_0_fun/ppermute | solution.py:285
  38.0 48.2 %collective-permute-start.11 = (f32[2,8,32,512]{3,2,1,0:T(8,128)S(1)}, f32[2,8,32,512]{3,2,1,0:T(8,128)}, u32[]{:S(2)}, u32[]{:S(2)}) collective-permute-start(f32[2,8,32,512]{3,2,1,0:T(8,128)S(1)} %get-tuple-element.175.refs_1_.refs_2_), channel_id=1, source_target_pairs={{0,1},{1,0},{2,3},{3,2},{4,5},{5,4},{6,7},{7,6},{8,9},{9,8},{10,11... | collective-permute-start | bytes 3145736 | tf_op jit(solution)/shard_map/cond/branch_0_fun/ppermute | solution.py:285
  39.4 3.2 %copy-start.25 = (f32[2,8,32,512]{3,2,1,0:T(8,128)}, f32[2,8,32,512]{3,2,1,0:T(8,128)S(1)}, u32[]{:S(2)}) copy-start(f32[2,8,32,512]{3,2,1,0:T(8,128)S(1)} %collective-permute-done.refs_2_.refs_1_) | copy-start | bytes 3145732 | tf_op jit(solution)/shard_map/cond
  39.4 66.3 %collective-permute-start.10 = (f32[2,8,32,512]{3,2,1,0:T(8,128)S(1)}, f32[2,8,32,512]{3,2,1,0:T(8,128)}, u32[]{:S(2)}, u32[]{:S(2)}) collective-permute-start(f32[2,8,32,512]{3,2,1,0:T(8,128)S(1)} %get-tuple-element.175.refs_1_.refs_2_), channel_id=1, source_target_pairs={{0,16},{8,24},{16,0},{24,8},{1,17},{9,25},{17,1},{25,9},{2,18},{10... | collective-permute-start | bytes 3145736 | tf_op jit(solution)/shard_map/cond/branch_0_fun/ppermute | solution.py:283
  41.6 1.0 copy-start.27
  51.1 64.3 %collective-permute-start.2 = (f32[28,64,128]{2,1,0:T(8,128)}, f32[28,64,128]{2,1,0:T(8,128)S(1)}, u32[]{:S(2)}, u32[]{:S(2)}) collective-permute-start(f32[28,64,128]{2,1,0:T(8,128)} %get-tuple-element.86), channel_id=1, source_target_pairs={{0,2},{6,4},{1,3},{7,5},{8,10},{14,12},{9,11},{15,13},{16,18},{22,... | collective-permute-start | bytes 2752520 | tf_op jit(solution)/shard_map/cond/branch_0_fun/ppermute | solution.py:316
  63.2 56.2 %collective-permute-start.15 = (f32[2,8,32,512]{3,2,1,0:T(8,128)}, f32[2,8,32,512]{3,2,1,0:T(8,128)}, u32[]{:S(2)}, u32[]{:S(2)}) collective-permute-start(f32[2,8,32,512]{3,2,1,0:T(8,128)} %collective-permute-done.5.refs_0_), channel_id=1, source_target_pairs={{0,1},{1,0},{2,3},{3,2},{4,5},{5,4},{6,7},{7,6},{8,9},{9,8},{10,11... | collective-permute-start | bytes 3145736 | tf_op jit(solution)/shard_map/cond/branch_0_fun/ppermute | solution.py:285
  86.2 33.2 %collective-permute-start.16 = (f32[2,8,32,512]{3,2,1,0:T(8,128)}, f32[2,8,32,512]{3,2,1,0:T(8,128)}, u32[]{:S(2)}, u32[]{:S(2)}) collective-permute-start(f32[2,8,32,512]{3,2,1,0:T(8,128)} %collective-permute-done.11.refs_1_), channel_id=1, source_target_pairs={{0,16},{8,24},{16,0},{24,8},{1,17},{9,25},{17,1},{25,9},{2,18},{10... | collective-permute-start | bytes 3145736 | tf_op jit(solution)/shard_map/cond/branch_0_fun/ppermute | solution.py:283
  101.3 29.0 %collective-permute-start.7 = (f32[28,64,128]{2,1,0:T(8,128)}, f32[28,64,128]{2,1,0:T(8,128)}, u32[]{:S(2)}, u32[]{:S(2)}) collective-permute-start(f32[28,64,128]{2,1,0:T(8,128)} %get-tuple-element.90), channel_id=1, source_target_pairs={{0,2},{6,4},{1,3},{7,5},{8,10},{14,12},{9,11},{15,13},{16,18},{22,... | collective-permute-start | bytes 2752520 | tf_op jit(solution)/shard_map/cond/branch_0_fun/ppermute | solution.py:316
  114.0 31.4 %collective-permute-start.12 = (f32[28,64,128]{2,1,0:T(8,128)}, f32[28,64,128]{2,1,0:T(8,128)S(1)}, u32[]{:S(2)}, u32[]{:S(2)}) collective-permute-start(f32[28,64,128]{2,1,0:T(8,128)} %get-tuple-element.94), channel_id=1, source_target_pairs={{0,2},{6,4},{1,3},{7,5},{8,10},{14,12},{9,11},{15,13},{16,18},{22,... | collective-permute-start | bytes 2752520 | tf_op jit(solution)/shard_map/cond/branch_0_fun/ppermute | solution.py:316
  115.4 12.4 %copy-start.13 = (f32[28,64,128]{2,1,0:T(8,128)}, f32[28,64,128]{2,1,0:T(8,128)S(1)}, u32[]{:S(2)}) copy-start(f32[28,64,128]{2,1,0:T(8,128)S(1)} %collective-permute-done.2.refs_1_) | copy-start | bytes 2752516 | tf_op jit(solution)/shard_map/cond
  117.8 12.6 %copy-start.34 = (f32[20,64,128]{2,1,0:T(8,128)S(1)}, f32[20,64,128]{2,1,0:T(8,128)}, u32[]{:S(2)}) copy-start(f32[20,64,128]{2,1,0:T(8,128)} %get-tuple-element.91) | copy-start | bytes 1966084 | tf_op jit(solution)/shard_map/cond
  117.8 29.5 %collective-permute-start.3 = (f32[20,64,128]{2,1,0:T(8,128)}, f32[20,64,128]{2,1,0:T(8,128)}, u32[]{:S(2)}, u32[]{:S(2)}) collective-permute-start(f32[20,64,128]{2,1,0:T(8,128)} %slice_add_fusion.3), channel_id=1, source_target_pairs={{2,4},{4,2},{3,5},{5,3},{10,12},{12,10},{11,13},{13,11},{18,20},{2... | collective-permute-start | bytes 1966088 | tf_op jit(solution)/shard_map/cond/branch_0_fun/ppermute | solution.py:316
  127.8 17.7 %copy-start.36 = (f32[20,64,128]{2,1,0:T(8,128)S(1)}, f32[20,64,128]{2,1,0:T(8,128)}, u32[]{:S(2)}) copy-start(f32[20,64,128]{2,1,0:T(8,128)} %get-tuple-element.95) | copy-start | bytes 1966084 | tf_op jit(solution)/shard_map/cond
  127.8 19.5 %copy-start.49 = (f32[11,64,128]{2,1,0:T(8,128)S(1)}, f32[11,64,128]{2,1,0:T(8,128)}, u32[]{:S(2)}) copy-start(f32[11,64,128]{2,1,0:T(8,128)} %get-tuple-element.88) | copy-start | bytes 1081348 | tf_op jit(solution)/shard_map/cond
  127.8 33.7 %collective-permute-start.17 = (f32[28,64,128]{2,1,0:T(8,128)}, f32[28,64,128]{2,1,0:T(8,128)S(1)}, u32[]{:S(2)}, u32[]{:S(2)}) collective-permute-start(f32[28,64,128]{2,1,0:T(8,128)} %get-tuple-element.98), channel_id=1, source_target_pairs={{0,2},{6,4},{1,3},{7,5},{8,10},{14,12},{9,11},{15,13},{16,18},{22,... | collective-permute-start | bytes 2752520 | tf_op jit(solution)/shard_map/cond/branch_0_fun/ppermute | solution.py:316
  130.3 20.0 %copy-start.51 = (f32[11,64,128]{2,1,0:T(8,128)S(1)}, f32[11,64,128]{2,1,0:T(8,128)}, u32[]{:S(2)}) copy-start(f32[11,64,128]{2,1,0:T(8,128)} %get-tuple-element.92) | copy-start | bytes 1081348 | tf_op jit(solution)/shard_map/cond
  131.6 29.9 %copy-start.35 = (f32[20,64,128]{2,1,0:T(8,128)S(1)}, f32[20,64,128]{2,1,0:T(8,128)}, u32[]{:S(2)}) copy-start(f32[20,64,128]{2,1,0:T(8,128)} %get-tuple-element.99) | copy-start | bytes 1966084 | tf_op jit(solution)/shard_map/cond
  131.6 18.8 %collective-permute-start.8 = (f32[20,64,128]{2,1,0:T(8,128)S(1)}, f32[20,64,128]{2,1,0:T(8,128)S(1)}, u32[]{:S(2)}, u32[]{:S(2)}) collective-permute-start(f32[20,64,128]{2,1,0:T(8,128)S(1)} %slice_add_fusion.2), channel_id=1, source_target_pairs={{2,4},{4,2},{3,5},{5,3},{10,12},{12,10},{11,13},{13,11},{18,20},{2... | collective-permute-start | bytes 1966088 | tf_op jit(solution)/shard_map/cond/branch_0_fun/ppermute | solution.py:316
  145.5 17.0 %copy-start.14 = (f32[28,64,128]{2,1,0:T(8,128)}, f32[28,64,128]{2,1,0:T(8,128)S(1)}, u32[]{:S(2)}) copy-start(f32[28,64,128]{2,1,0:T(8,128)S(1)} %collective-permute-done.12.refs_1_) | copy-start | bytes 2752516 | tf_op jit(solution)/shard_map/cond
  146.5 17.6 %copy-start.64 = (s32[3]{0:T(128)S(1)}, s32[3]{0:T(128)}, u32[]{:S(2)}) copy-start(s32[3]{0:T(128)} %constant.85) | copy-start | bytes 40 | tf_op jit(solution)/shard_map/cond
  146.5 26.6 %collective-permute-start.13 = (f32[20,64,128]{2,1,0:T(8,128)}, f32[20,64,128]{2,1,0:T(8,128)S(1)}, u32[]{:S(2)}, u32[]{:S(2)}) collective-permute-start(f32[20,64,128]{2,1,0:T(8,128)} %slice_add_fusion.1), channel_id=1, source_target_pairs={{2,4},{4,2},{3,5},{5,3},{10,12},{12,10},{11,13},{13,11},{18,20},{2... | collective-permute-start | bytes 1966088 | tf_op jit(solution)/shard_map/cond/branch_0_fun/ppermute | solution.py:316
  149.1 15.7 %collective-permute-start.4 = (f32[11,64,128]{2,1,0:T(8,128)}, f32[11,64,128]{2,1,0:T(8,128)}, u32[]{:S(2)}, u32[]{:S(2)}) collective-permute-start(f32[11,64,128]{2,1,0:T(8,128)} %slice_add_fusion.7), channel_id=1, source_target_pairs={{4,6},{2,0},{5,7},{3,1},{12,14},{10,8},{13,15},{11,9},{20,22},{18,... | collective-permute-start | bytes 1081352 | tf_op jit(solution)/shard_map/cond/branch_0_fun/ppermute | solution.py:316
  150.4 14.6 %copy-start.22 = (f32[20,64,128]{2,1,0:T(8,128)}, f32[20,64,128]{2,1,0:T(8,128)S(1)}, u32[]{:S(2)}) copy-start(f32[20,64,128]{2,1,0:T(8,128)S(1)} %collective-permute-done.8.refs_6_) | copy-start | bytes 1966084 | tf_op jit(solution)/shard_map/cond
  151.2 13.7 %collective-permute-start.9 = (f32[11,64,128]{2,1,0:T(8,128)}, f32[11,64,128]{2,1,0:T(8,128)S(1)}, u32[]{:S(2)}, u32[]{:S(2)}) collective-permute-start(f32[11,64,128]{2,1,0:T(8,128)} %slice_add_fusion.6), channel_id=1, source_target_pairs={{4,6},{2,0},{5,7},{3,1},{12,14},{10,8},{13,15},{11,9},{20,22},{18,... | collective-permute-start | bytes 1081352 | tf_op jit(solution)/shard_map/cond/branch_0_fun/ppermute | solution.py:316
  161.5 7.8 %copy-start.15 = (f32[28,64,128]{2,1,0:T(8,128)}, f32[28,64,128]{2,1,0:T(8,128)S(1)}, u32[]{:S(2)}) copy-start(f32[28,64,128]{2,1,0:T(8,128)S(1)} %collective-permute-done.17.refs_5_) | copy-start | bytes 2752516 | tf_op jit(solution)/shard_map/cond
  162.5 11.9 %collective-permute-start.18 = (f32[20,64,128]{2,1,0:T(8,128)}, f32[20,64,128]{2,1,0:T(8,128)}, u32[]{:S(2)}, u32[]{:S(2)}) collective-permute-start(f32[20,64,128]{2,1,0:T(8,128)} %slice_add_fusion), channel_id=1, source_target_pairs={{2,4},{4,2},{3,5},{5,3},{10,12},{12,10},{11,13},{13,11},{18,20},{2... | collective-permute-start | bytes 1966088 | tf_op jit(solution)/shard_map/cond/branch_0_fun/ppermute | solution.py:316
  165.0 0.7 copy-start.52
  169.3 3.7 %copy-start.48 = (f32[11,64,128]{2,1,0:T(8,128)S(1)}, f32[11,64,128]{2,1,0:T(8,128)}, u32[]{:S(2)}) copy-start(f32[11,64,128]{2,1,0:T(8,128)} %get-tuple-element.96) | copy-start | bytes 1081348 | tf_op jit(solution)/shard_map/cond
  169.3 5.1 %copy-start.50 = (f32[11,64,128]{2,1,0:T(8,128)S(1)}, f32[11,64,128]{2,1,0:T(8,128)}, u32[]{:S(2)}) copy-start(f32[11,64,128]{2,1,0:T(8,128)} %get-tuple-element.100) | copy-start | bytes 1081348 | tf_op jit(solution)/shard_map/cond
  169.3 30.2 %all-to-all-start = ((f32[8,2,2,64,128]{4,3,2,1,0:T(8,128)}), f32[8,2,2,64,128]{4,3,2,1,0:T(8,128)S(1)}, u32[]{:S(2)}, u32[]{:S(2)}) async-start(f32[8,2,2,64,128]{4,3,2,1,0:T(8,128)} %branch_0_fun.11), calls=%async_computation | async-start | bytes 2097152 | tf_op jit(solution)/shard_map/cond/branch_0_fun/all_to_all | solution.py:321
  173.0 22.2 %copy-start.21 = (f32[20,64,128]{2,1,0:T(8,128)}, f32[20,64,128]{2,1,0:T(8,128)S(1)}, u32[]{:S(2)}) copy-start(f32[20,64,128]{2,1,0:T(8,128)S(1)} %collective-permute-done.13.refs_2_) | copy-start | bytes 1966084 | tf_op jit(solution)/shard_map/cond
  173.1 14.7 %collective-permute-start.14 = (f32[11,64,128]{2,1,0:T(8,128)S(1)}, f32[11,64,128]{2,1,0:T(8,128)S(1)}, u32[]{:S(2)}, u32[]{:S(2)}) collective-permute-start(f32[11,64,128]{2,1,0:T(8,128)S(1)} %slice_add_fusion.5), channel_id=1, source_target_pairs={{4,6},{2,0},{5,7},{3,1},{12,14},{10,8},{13,15},{11,9},{20,22},{18,... | collective-permute-start | bytes 1081352 | tf_op jit(solution)/shard_map/cond/branch_0_fun/ppermute | solution.py:316
  175.5 19.7 %collective-permute-start.19 = (f32[11,64,128]{2,1,0:T(8,128)S(1)}, f32[11,64,128]{2,1,0:T(8,128)S(1)}, u32[]{:S(2)}, u32[]{:S(2)}) collective-permute-start(f32[11,64,128]{2,1,0:T(8,128)S(1)} %slice_add_fusion.4), channel_id=1, source_target_pairs={{4,6},{2,0},{5,7},{3,1},{12,14},{10,8},{13,15},{11,9},{20,22},{18,... | collective-permute-start | bytes 1081352 | tf_op jit(solution)/shard_map/cond/branch_0_fun/ppermute | solution.py:316
  187.8 7.4 %copy-start.53 = (f32[11,64,128]{2,1,0:T(8,128)}, f32[11,64,128]{2,1,0:T(8,128)S(1)}, u32[]{:S(2)}) copy-start(f32[11,64,128]{2,1,0:T(8,128)S(1)} %collective-permute-done.14.refs_3_) | copy-start | bytes 1081348 | tf_op jit(solution)/shard_map/cond
  195.2 0.7 copy-start.54
  199.5 19.6 %copy-start.4 = (f32[8,2,2,64,128]{4,3,2,1,0:T(8,128)}, f32[8,2,2,64,128]{4,3,2,1,0:T(8,128)S(1)}, u32[]{:S(2)}) copy-start(f32[8,2,2,64,128]{4,3,2,1,0:T(8,128)S(1)} %all-to-all-done.refs_0_) | copy-start | bytes 3145732 | tf_op jit(solution)/shard_map/cond
  221.1 1.3 copy-start.18
